TPU v7x, 32 devices: a 4x4x1 block of a 4x4x8 slice. The times are simulated.
32 devices in a mesh: dp: 1 (over z), tp: 4 (over y), sp: 8 (over x, core).
Axes of the slice: x: 4, y: 4, z: 1, core: 2. Of those that a mesh axis runs over, the one named last changes fastest.
The devices are a block of a 4x4x8 slice.
Arguments:
- tokens: bfloat16 [32, 2048], P(('dp', 'sp'))
- states: float32 [8, 32, 32, 64, 64], P('sp', 'dp', 'tp')
- k_cache: bfloat16 [32, 8, 8192, 64], P('dp', 'tp', 'sp')
- v_cache: bfloat16 [32, 8, 8192, 64], P('dp', 'tp', 'sp')
- slopes: float32 [32], P('tp')
- lin_gain: float32 [2048], replicated
- w_lin_qkv: bfloat16 [2048, 3, 2048], P(None, None, 'tp')
- w_lin_gate: bfloat16 [2048, 2048], P(None, 'tp')
- out_gain: float32 [2048], P('tp')
- w_lin_out: bfloat16 [2048, 2048], P('tp')
- attn_gain: float32 [2048], replicated
- w_attn_in: bfloat16 [2048, 8, 6, 64], P(None, 'tp')
- w_attn_out: bfloat16 [2048, 2048], P('tp')
Outputs:
- output 1: bfloat16 [32, 2048], P(('dp', 'sp'))
- output 2: float32 [32, 32, 64, 64], P(('dp', 'sp'), 'tp')
- output 3: bfloat16 [32, 8, 8208, 64], P(('dp', 'sp'), 'tp')
- output 4: bfloat16 [32, 8, 8208, 64], P(('dp', 'sp'), 'tp')
All inputs are finite; a program needn't handle non-finite values.
Results may differ from a plain program's by a relative error of at most 0.0127504.
Values are sent between devices in bfloat16 or wider.
A program may use at most 768 MiB of HBM per device.

v0:
```python
import jax
import jax.numpy as jnp
from jax import lax
from jax.sharding import PartitionSpec as P

NORM_EPS = 1e-6
ROPE_BASE = 10000000.0
RES_ALPHA = 1.0
RES_BETA = 1.0
CACHE_EXTRA = 16


def rms_norm(vals_in, gain_vec):
    vals32 = vals_in.astype(jnp.float32)
    inv_rms = lax.rsqrt(jnp.mean(vals32 * vals32, axis=-1, keepdims=True) + NORM_EPS)
    return vals32 * inv_rms * gain_vec


def rotary(vals_in, position):
    rope_dim = vals_in.shape[-1] // 2
    half_dim = rope_dim // 2
    inv_freq = ROPE_BASE ** (-jnp.arange(0, rope_dim, 2, dtype=jnp.float32) / rope_dim)
    angles = position * inv_freq
    cosine = jnp.cos(angles)
    sine_vals = jnp.sin(angles)
    vals32 = vals_in.astype(jnp.float32)
    first_half = vals32[..., :half_dim]
    second_half = vals32[..., half_dim:rope_dim]
    return jnp.concatenate([first_half * cosine - second_half * sine_vals, second_half * cosine + first_half * sine_vals, vals32[..., rope_dim:]], axis=-1).astype(jnp.bfloat16)


def lightning_layer(tokens, moved_state, slopes, lin_gain, w_lin_qkv, w_lin_gate, out_gain, w_lin_out, hidden_width):
    rows = tokens.shape[0]
    heads_dev = slopes.shape[0]
    head_dim = moved_state.shape[-1]
    normed = rms_norm(tokens, lin_gain).astype(jnp.bfloat16)
    lin_proj = jnp.einsum('bd,dkn->bkn', normed, w_lin_qkv, preferred_element_type=jnp.float32)
    act_vals = jax.nn.silu(lin_proj).astype(jnp.bfloat16).reshape(rows, 3, heads_dev, head_dim)
    state_new = jnp.exp(-slopes)[None, :, None, None] * moved_state + jnp.einsum('bhd,bhe->bhde', act_vals[:, 1], act_vals[:, 2], preferred_element_type=jnp.float32)
    lin_attn = jnp.einsum('bhd,bhde->bhe', act_vals[:, 0].astype(jnp.float32), state_new).reshape(rows, heads_dev * head_dim)
    square_sum = lax.psum(jnp.sum(lin_attn * lin_attn, axis=-1, keepdims=True), 'tp')
    inv_rms = lax.rsqrt(square_sum / hidden_width + NORM_EPS)
    gate_vals = jax.nn.sigmoid(jnp.dot(normed, w_lin_gate, preferred_element_type=jnp.float32))
    mixed_out = (lin_attn * inv_rms * out_gain * gate_vals).astype(jnp.bfloat16)
    lin_out = lax.psum(jnp.dot(mixed_out, w_lin_out, preferred_element_type=jnp.float32), 'tp')
    hidden = (RES_ALPHA * normed.astype(jnp.float32) + RES_BETA * lin_out).astype(jnp.bfloat16)
    return hidden, state_new


def solution(mesh):
    seq_shards = mesh.shape['sp']
    tp_size = mesh.shape['tp']

    def device_step(tokens, states, k_cache, v_cache, slopes, lin_gain, w_lin_qkv, w_lin_gate, out_gain, w_lin_out, attn_gain, w_attn_in, w_attn_out):
        rows = tokens.shape[0]
        kv_dev = k_cache.shape[1]
        shard_len = k_cache.shape[2]
        head_dim = k_cache.shape[3]
        group = w_attn_in.shape[2] - 2
        prompt_len = seq_shards * shard_len
        k_moved = lax.all_to_all(k_cache, 'sp', 0, 2, tiled=True)
        v_moved = lax.all_to_all(v_cache, 'sp', 0, 2, tiled=True)
        shard_idx = lax.axis_index('sp')
        offset = (shard_len * (seq_shards - 1 - shard_idx)).astype(jnp.float32)
        weighted = states[0] * jnp.exp(-slopes * offset)[None, :, None, None]
        moved_state = lax.psum_scatter(weighted, 'sp', scatter_dimension=0, tiled=True)
        hidden, state_new = lightning_layer(tokens, moved_state, slopes, lin_gain, w_lin_qkv, w_lin_gate, out_gain, w_lin_out, tp_size * slopes.shape[0] * head_dim)

        normed = rms_norm(hidden, attn_gain).astype(jnp.bfloat16)
        attn_proj = jnp.einsum('bd,dkjn->bkjn', normed, w_attn_in, preferred_element_type=jnp.float32).astype(jnp.bfloat16)
        query_rot = rotary(attn_proj[:, :, :group], prompt_len)
        key_new = rotary(attn_proj[:, :, group], prompt_len)
        value_new = attn_proj[:, :, group + 1]
        score_scale = head_dim ** -0.5
        scores = jnp.einsum('bkgd,bktd->bkgt', query_rot, k_moved, preferred_element_type=jnp.float32) * score_scale
        new_score = jnp.einsum('clhe,cle->clh', query_rot, key_new, preferred_element_type=jnp.float32) * score_scale
        row_max = jnp.maximum(jnp.max(scores, axis=-1), new_score)
        probs = jnp.exp(scores - row_max[..., None])
        new_prob = jnp.exp(new_score - row_max)
        prob_sum = jnp.sum(probs, axis=-1) + new_prob
        weighted_sum = jnp.einsum('bkgt,bktd->bkgd', probs.astype(jnp.bfloat16), v_moved, preferred_element_type=jnp.float32)
        weighted_sum = weighted_sum + new_prob.astype(jnp.bfloat16).astype(jnp.float32)[..., None] * value_new.astype(jnp.float32)[:, :, None, :]
        head_out = (weighted_sum / prob_sum[..., None]).astype(jnp.bfloat16).reshape(rows, kv_dev * group * head_dim)
        attn_out = lax.psum(jnp.dot(head_out, w_attn_out, preferred_element_type=jnp.float32), 'tp')
        hidden_out = (RES_ALPHA * normed.astype(jnp.float32) + RES_BETA * attn_out).astype(jnp.bfloat16)
        tail_zeros = jnp.zeros((rows, kv_dev, CACHE_EXTRA - 1, head_dim), jnp.bfloat16)
        k_out = jnp.concatenate([k_moved, key_new[:, :, None, :], tail_zeros], axis=2)
        v_out = jnp.concatenate([v_moved, value_new[:, :, None, :], tail_zeros], axis=2)
        return hidden_out, state_new, k_out, v_out

    batch_spec = P(('dp', 'sp'), None)
    head_spec = P(('dp', 'sp'), 'tp', None, None)
    cache_spec = P('dp', 'tp', 'sp', None)
    in_specs = (batch_spec, P('sp', 'dp', 'tp', None, None), cache_spec, cache_spec, P('tp'), P(None), P(None, None, 'tp'), P(None, 'tp'), P('tp'), P('tp', None), P(None), P(None, 'tp', None, None), P('tp', None))
    out_specs = (batch_spec, head_spec, head_spec, head_spec)
    return jax.shard_map(device_step, mesh=mesh, in_specs=in_specs, out_specs=out_specs, check_vma=False)
```

profile of v0, /device:TPU:96, one launch (start us, length us, event | category | flops | bytes accessed | tf_op | source)
XLA Modules:
  0.0 371.2 jit_solution(6357733089299862186)
XLA Ops:
  7.2 0.0 copy-start
  7.2 5.4 %all-to-all-start.1 = ((bf16[32,2,1024,64]{2,3,1,0:T(8,128)(2,1)}), bf16[32,2,1024,64]{2,3,1,0:T(8,128)(2,1)}, u32[]{:S(2)}, u32[]{:S(2)}) async-start(bf16[32,2,1024,64]{2,3,1,0:T(8,128)(2,1)} %param.16), calls=%async_computation.2 | async-start | bytes 16777216 | tf_op jit(solution)/shard_map/all_to_all | solution.py:62
  12.7 0.1 reduce-scatter.2.cloned.1.call-start
  12.8 8.8 %bitcast_multiply_fusion = f32[32,8,64,64]{3,2,1,0:T(8,128)} fusion(f32[1,32,8,64,64]{4,3,2,1,0:T(8,128)} %param.14, f32[8]{0:T(128)S(1)} %get-tuple-element.17), kind=kLoop, calls=%fused_computation.1 | loop fusion | flops 1048576 | bytes 8388640 | tf_op jit(solution)/shard_map/mul | solution.py:65
  21.5 0.1 reduce-scatter.2.cloned.1.call-update
  21.6 122.0 %all-to-all-done.1 = bf16[32,2,1024,64]{2,3,1,0:T(8,128)(2,1)} async-done(((bf16[32,2,1024,64]{2,3,1,0:T(8,128)(2,1)}), bf16[32,2,1024,64]{2,3,1,0:T(8,128)(2,1)}, u32[]{:S(2)}, u32[]{:S(2)}) %all-to-all-start.1) | async-done | bytes 8388640 | tf_op jit(solution)/shard_map/all_to_all | solution.py:62
  143.6 5.2 %all-to-all-start = ((bf16[32,2,1024,64]{2,3,1,0:T(8,128)(2,1)}), bf16[32,2,1024,64]{2,3,1,0:T(8,128)(2,1)}, u32[]{:S(2)}, u32[]{:S(2)}) async-start(bf16[32,2,1024,64]{2,3,1,0:T(8,128)(2,1)} %param.15), calls=%async_computation.1 | async-start | bytes 16777216 | tf_op jit(solution)/shard_map/all_to_all | solution.py:61
  148.9 0.1 fusion.12
  149.0 3.8 %fusion.18 = bf16[4,3,512]{2,0,1:T(4,128)(2,1)S(1)} fusion(bf16[2048,3,512]{2,0,1:T(8,128)(2,1)} %param.19, bf16[4,2048]{1,0:T(4,128)(2,1)S(1)} %copy-done.2, f32[2048]{0:T(1024)S(1)} %copy-done.3, f32[4]{0:T(128)S(1)} %add_rsqrt_fusion.1), kind=kOutput, calls=%fused_computation.33 | convolution fusion | flops 25229312 | bytes 6328336 | tf_op jit(solution)/shard_map/bd,dkn->bkn/dot_general | solution.py:37
  152.8 0.1 reshape.120
  152.9 0.1 fusion.35
  153.0 12.1 %copy.56 = bf16[8,4,2,1024,64]{3,0,4,2,1:T(8,128)(2,1)} copy(bf16[8,4,2,1024,64]{3,4,2,1,0:T(8,128)(2,1)} %bitcast.19) | data formatting | bytes 16777216 | tf_op jit(solution)/shard_map/all_to_all | solution.py:62
  165.1 13.5 %all_to_all.33 = bf16[4,2,8192,64]{2,3,1,0:T(8,128)(2,1)} reshape(bf16[4,2,8,1024,64]{3,2,4,1,0:T(8,128)(2,1)} %bitcast.71) | data formatting | bytes 16777216 | tf_op jit(solution)/shard_map/all_to_all | solution.py:62
  178.5 64.7 %all-to-all-done = bf16[32,2,1024,64]{2,3,1,0:T(8,128)(2,1)} async-done(((bf16[32,2,1024,64]{2,3,1,0:T(8,128)(2,1)}), bf16[32,2,1024,64]{2,3,1,0:T(8,128)(2,1)}, u32[]{:S(2)}, u32[]{:S(2)}) %all-to-all-start) | async-done | bytes 8388640 | tf_op jit(solution)/shard_map/all_to_all | solution.py:61
  243.2 12.1 %copy.57 = bf16[8,4,2,1024,64]{3,0,4,2,1:T(8,128)(2,1)} copy(bf16[8,4,2,1024,64]{3,4,2,1,0:T(8,128)(2,1)} %bitcast.12) | data formatting | bytes 16777216 | tf_op jit(solution)/shard_map/all_to_all | solution.py:61
  255.3 13.5 %all_to_all.29 = bf16[4,2,8192,64]{2,3,1,0:T(8,128)(2,1)} reshape(bf16[4,2,8,1024,64]{3,2,4,1,0:T(8,128)(2,1)} %bitcast.72) | data formatting | bytes 16777216 | tf_op jit(solution)/shard_map/all_to_all | solution.py:61
  268.8 1.6 multiply_add_fusion
  270.4 0.0 copy-start.1
  270.4 1.0 copy-done.1
  271.4 0.2 fusion.21
  271.6 0.1 reshape.123
  271.7 0.1 multiply_reduce_fusion
  271.8 12.4 %psum.21 = f32[4,1]{0,1:T(1,128)S(1)} all-reduce(f32[4,1]{0,1:T(1,128)S(1)} %bitcast.79), channel_id=1, replica_groups=mesh['dp'=1,'tp'=4,'sp'=8] {'tp'}, use_global_device_ids=true, to_apply=%region_3.4 | all-reduce | flops 4 | bytes 32 | tf_op jit(solution)/shard_map/psum | solution.py:41
  284.3 3.0 fusion.7
  287.3 14.5 %psum.22 = f32[4,2048]{1,0:T(4,128)S(1)} all-reduce(f32[4,2048]{1,0:T(4,128)S(1)} %fusion.7), channel_id=1, replica_groups=mesh['dp'=1,'tp'=4,'sp'=8] {'tp'}, use_global_device_ids=true, to_apply=%region_4.5 | all-reduce | flops 8192 | bytes 65536 | tf_op jit(solution)/shard_map/psum | solution.py:45
  301.8 0.2 fusion.15
  302.0 0.1 fusion.17
  302.1 1.3 convolution_convert_fusion
  303.4 0.1 slice.56
  303.5 0.1 slice.83
  303.6 0.1 slice_bitcast_fusion.4
  303.6 0.1 subtract_convert_fusion.1
  303.7 0.1 subtract_convert_fusion
  303.8 0.1 pad_maximum_fusion
  303.9 4.7 %fusion.43 = (f32[4,2,4]{2,1,0:T(2,128)S(1)}, f32[4,2,4,8192]{3,2,1,0:T(4,128)S(1)}) fusion(bf16[4,2,8192,64]{2,3,1,0:T(8,128)(2,1)} %all_to_all.29, bf16[4,2,4,64]{3,0,2,1:T(4,128)(2,1)S(1)} %pad_maximum_fusion), kind=kOutput, calls=%fused_computation.79 | convolution fusion | flops 34078688 | bytes 9441408 | tf_op jit(solution)/shard_map/bkgd,bktd->bkgt/dot_general | solution.py:75
  308.6 0.1 maximum_bitcast_fusion
  308.6 0.1 fusion.27
  308.8 0.5 fusion.8
  309.3 5.7 %fusion.1 = bf16[4,2,4,64]{3,2,1,0:T(4,128)(2,1)S(1)} fusion(bf16[4,2,8192,64]{2,3,1,0:T(8,128)(2,1)} %all_to_all.33, f32[4,2,4,8192]{3,2,1,0:T(4,128)S(1)} %get-tuple-element.19, f32[4,2,4]{2,1,0:T(2,128)S(1)} %multiply_maximum_fusion, f32[4,2,4]{2,1,0:T(2,128)S(1)} %get-tuple-element.13, f32[4,2,64]{2,1,0:T(2,128)S(1)} %copy.30, ...), kind=kOutput, calls=%fused_computation.7 | convolution fusion | flops 34086912 | bytes 9443712 | tf_op jit(solution)/shard_map/bkgt,bktd->bkgd/dot_general | solution.py:81
  315.0 0.1 reshape.124
  315.1 2.0 fusion.44
  317.1 16.3 %psum.23 = f32[4,2048]{1,0:T(4,128)S(1)} all-reduce(f32[4,2048]{1,0:T(4,128)S(1)} %fusion.44), channel_id=1, replica_groups=mesh['dp'=1,'tp'=4,'sp'=8] {'tp'}, use_global_device_ids=true, to_apply=%region_8.9 | all-reduce | flops 8192 | bytes 65536 | tf_op jit(solution)/shard_map/psum | solution.py:84
  333.4 0.6 add_convert_fusion
  334.1 0.1 pad_maximum_fusion.1
  334.1 0.2 copy.35
  334.3 0.2 copy.36
  334.5 14.9 %concatenate.36 = bf16[4,2,8208,64]{2,3,1,0:T(8,128)(2,1)} concatenate(bf16[4,2,8192,64]{2,3,1,0:T(8,128)(2,1)} %all_to_all.29, bf16[4,2,1,64]{2,3,1,0:T(8,128)(2,1)S(1)} %copy.35, bf16[4,2,15,64]{2,3,1,0:T(8,128)(2,1)S(1)} %broadcast_in_dim.5), dimensions={2} | concatenate | bytes 16809984 | tf_op jit(solution)/shard_map/concatenate | solution.py:87
  349.4 14.9 %concatenate.37 = bf16[4,2,8208,64]{2,3,1,0:T(8,128)(2,1)} concatenate(bf16[4,2,8192,64]{2,3,1,0:T(8,128)(2,1)} %all_to_all.33, bf16[4,2,1,64]{2,3,1,0:T(8,128)(2,1)S(1)} %copy.36, bf16[4,2,15,64]{2,3,1,0:T(8,128)(2,1)S(1)} %broadcast_in_dim.5), dimensions={2} | concatenate | bytes 16809984 | tf_op jit(solution)/shard_map/concatenate | solution.py:88
  (23 shorter events, 0.1 us)
Async XLA Ops:
  7.2 294.9 %copy-start = (bf16[2048,2,6,64]{0,3,2,1:T(8,128)(2,1)S(1)}, bf16[2048,2,6,64]{0,3,2,1:T(8,128)(2,1)}, u32[]{:S(2)}) copy-start(bf16[2048,2,6,64]{0,3,2,1:T(8,128)(2,1)} %param.24) | copy-start | bytes 9437188
  7.2 5.5 %copy-start.6 = (f32[8]{0:T(128)S(1)}, f32[8]{0:T(128)}, u32[]{:S(2)}) copy-start(f32[8]{0:T(128)} %param.17) | copy-start | bytes 100
  7.2 136.4 %all-to-all-start.1 = ((bf16[32,2,1024,64]{2,3,1,0:T(8,128)(2,1)}), bf16[32,2,1024,64]{2,3,1,0:T(8,128)(2,1)}, u32[]{:S(2)}, u32[]{:S(2)}) async-start(bf16[32,2,1024,64]{2,3,1,0:T(8,128)(2,1)} %param.16), calls=%async_computation.2 | async-start | bytes 16777216 | tf_op jit(solution)/shard_map/all_to_all | solution.py:62
  12.7 256.2 %reduce-scatter.2.cloned.1.call-start = ((), (), s32[]{:S(2)}) async-start(), calls=%async_computation.3 | async-start | bytes 9437184 | tf_op jit(solution)/shard_map/reduce_scatter | solution.py:66
  21.6 127.3 %copy-start.2 = (bf16[4,2048]{1,0:T(4,128)(2,1)S(1)}, bf16[4,2048]{1,0:T(4,128)(2,1)}, u32[]{:S(2)}) copy-start(bf16[4,2048]{1,0:T(4,128)(2,1)} %param.13) | copy-start | bytes 49156
  21.6 127.4 %copy-start.3 = (f32[2048]{0:T(1024)S(1)}, f32[2048]{0:T(1024)}, u32[]{:S(2)}) copy-start(f32[2048]{0:T(1024)} %param.18) | copy-start | bytes 24580
  143.6 99.6 %all-to-all-start = ((bf16[32,2,1024,64]{2,3,1,0:T(8,128)(2,1)}), bf16[32,2,1024,64]{2,3,1,0:T(8,128)(2,1)}, u32[]{:S(2)}, u32[]{:S(2)}) async-start(bf16[32,2,1024,64]{2,3,1,0:T(8,128)(2,1)} %param.15), calls=%async_computation.1 | async-start | bytes 16777216 | tf_op jit(solution)/shard_map/all_to_all | solution.py:61
  255.3 28.9 %copy-start.5 = (f32[512]{0:T(512)S(1)}, f32[512]{0:T(512)}, u32[]{:S(2)}) copy-start(f32[512]{0:T(512)} %param.21) | copy-start | bytes 6148
  255.3 46.6 %copy-start.4 = (f32[2048]{0:T(1024)S(1)}, f32[2048]{0:T(1024)}, u32[]{:S(2)}) copy-start(f32[2048]{0:T(1024)} %param.23) | copy-start | bytes 24580
  270.4 1.0 copy-start.1
Sparse Core Ops, SparseCore 0:
  21.7 125.2 reduce-scatter.1
where the time goes:
time: 373 us; the launch traced here: 371 us
  waiting for transfers between devices  187 us (50%)
  local copies, waits for them, and re-layouts  82.8 us (22%)
  blocking collectives  43.2 us (12%)
  matrix products  20.8 us (6%)
  between operations  14.3 us (4%)
  other arithmetic  12.5 us (3%)
  starting transfers between devices  10.7 us (3%)
    all_to_all x1, waiting for transfers between devices, device_step(): v_moved = lax.all_to_all(v_cache, 'sp', 0, 2, tiled=True)  122 us
    all_to_all x1, waiting for transfers between devices, device_step(): k_moved = lax.all_to_all(k_cache, 'sp', 0, 2, tiled=True)  64.7 us
    all_to_all x2, local copies, waits for them, and re-layouts, device_step(): k_moved = lax.all_to_all(k_cache, 'sp', 0, 2, tiled=True)  25.6 us
    all_to_all x2, local copies, waits for them, and re-layouts, device_step(): v_moved = lax.all_to_all(v_cache, 'sp', 0, 2, tiled=True)  25.6 us
    psum x1, blocking collectives, device_step(): lax.psum(jnp.dot(head_out, w_attn_out, preferred_element_type=jnp.float32...  16.3 us
    concatenate x1, local copies, waits for them, and re-layouts, device_step(): jnp.concatenate([k_moved, key_new[:, :, None, :], tail_zeros], axis=2)  14.9 us
    concatenate x1, local copies, waits for them, and re-layouts, device_step(): jnp.concatenate([v_moved, value_new[:, :, None, :], tail_zeros], axis=2)  14.9 us
    psum x1, blocking collectives, lightning_layer(): lax.psum(jnp.dot(mixed_out, w_lin_out, preferred_element_type=jnp.float32...  14.5 us
  transfers between devices with their start and end apart: 3, of which 2 were waited for; matrix products, arithmetic and copies ran while one was open for 10% of the time, Pallas kernels for 0%

commit v1 on v0

v1 whole, which is shorter than its diff:
```python
import functools

import numpy as np

import jax
import jax.numpy as jnp
from jax import lax
from jax.experimental import pallas as pl
from jax.experimental.pallas import tpu as pltpu
from jax.sharding import PartitionSpec as P

NORM_EPS = 1e-6
ROPE_BASE = 10000000.0
CACHE_EXTRA = 16
LANES = 128
F32 = jnp.float32
BF16 = jnp.bfloat16
MESH = pl.DeviceIdType.MESH
NT = (((1,), (1,)), ((), ()))


def rope_tables(kv_dev, segments, group, head_dim, position):
    rope_dim = head_dim // 2
    half = rope_dim // 2
    exponents = -np.arange(0, rope_dim, 2, dtype=np.float32) / np.float32(rope_dim)
    angles = (np.float32(position) * np.float32(ROPE_BASE) ** exponents).astype(np.float32)
    cosine, sine = np.cos(angles), np.sin(angles)
    table = np.zeros((8, kv_dev, segments, head_dim), np.float32)
    table[0] = 1.0
    for segment in range(group + 1):
        table[0, :, segment, :half] = cosine
        table[0, :, segment, half:rope_dim] = cosine
        table[1, :, segment, half:rope_dim] = sine
        table[2, :, segment, :half] = -sine
    return table.reshape(8, kv_dev * segments * head_dim)


def step_kernel(dims, tok, slopes, lin_gain, out_gain, attn_gain, rope, states, k_in, v_in, w_qkv, w_gate, w_lo, w_in, w_ao,
                hid_out, st_out, k_land, v_land,
                wv_qkv, wv_gate, wv_lo, wv_in, wv_ao, st_buf, p_out, p_in, acc, rs_in, sq_x, y_x, a_x, q_x, pr_out, pr_in,
                k_buf, v_buf, o_s, q_s, kn_s, vn_s, ho_s,
                w_sem, st_sem, pair_sem, rs_sem, sq_sem, y_sem, a_sem, q_sem, pr_sem, kv_send, kv_recv, own_sem, kb_sem):
    chips, tp_size, rows, heads, head_dim, kv_dev, group, shard_len = dims
    sp_size = 2 * chips
    pairs = heads // 2
    width = heads * head_dim
    model = tok.shape[1]
    hidden_width = tp_size * width
    segments = group + 2
    qrows = kv_dev * group * rows

    me = lax.axis_index("sp")
    me_tp = lax.axis_index("tp")
    chip = me // 2
    core = lax.rem(me, 2)
    peers = [(dc, cr) for dc, cr in ((2, 0), (1, 0), (3, 0), (2, 1), (1, 1), (3, 1), (0, 1))]

    def peer_index(dc, cr):
        return lax.rem(chip + dc, chips) * 2 + (core if cr == 0 else 1 - core)

    barrier = pltpu.get_barrier_semaphore()
    for dc, cr in peers:
        pl.semaphore_signal(barrier, inc=1, device_id={"sp": peer_index(dc, cr)}, device_id_type=MESH)
    for dt in range(1, tp_size):
        pl.semaphore_signal(barrier, inc=1, device_id={"tp": lax.rem(me_tp + dt, tp_size)}, device_id_type=MESH)
    pl.semaphore_wait(barrier, len(peers) + tp_size - 1)

    def remote(src, dst, send, recv, device):
        return pltpu.make_async_remote_copy(src_ref=src, dst_ref=dst, send_sem=send, recv_sem=recv, device_id=device, device_id_type=MESH)

    my_cols = pl.ds(pl.multiple_of(me * shard_len, LANES), shard_len)

    def kv_copies(round_idx):
        cache, land = ((k_in, k_land), (v_in, v_land))[round_idx % 2]
        row = round_idx // 2
        copies = []
        for n, (dc, cr) in enumerate(peers):
            dst = peer_index(dc, cr)
            copies.append(remote(cache.at[dst * rows + row], land.at[row, :, :, my_cols], kv_send.at[round_idx, n], kv_recv.at[round_idx, n], {"sp": dst}))
        return copies

    all_kv = []

    def start_round(round_idx):
        copies = kv_copies(round_idx)
        for copy in copies:
            copy.start()
        all_kv.extend(copies)

    start_round(0)

    def state_copy(step, slot):
        target_core = jnp.where(step < chips, 1 - core, core)
        dest = lax.rem(step, chips) * 2 + target_core
        return pltpu.make_async_copy(states.at[0, pl.ds(dest * rows, rows)], st_buf.at[slot], st_sem.at[slot])

    state_copy(0, 0).start()
    weight_copies = [pltpu.make_async_copy(src, dst, w_sem.at[n]) for n, (src, dst) in enumerate(
        ((w_qkv, wv_qkv), (w_gate, wv_gate), (w_lo, wv_lo), (w_in, wv_in), (w_ao, wv_ao)))]
    for copy in weight_copies:
        copy.start()

    lane = lax.broadcasted_iota(jnp.int32, (1, LANES), 1)
    low_half = lane < head_dim

    def pair_slope(p):
        return jnp.where(low_half, jnp.full((1, LANES), slopes[2 * p], F32), jnp.full((1, LANES), slopes[2 * p + 1], F32))

    offset = (shard_len * (sp_size - 1 - me)).astype(F32)
    decay = [jnp.exp(-pair_slope(p) * offset) for p in range(pairs)]

    def weigh_step(step, target):
        slot = lax.rem(step, 2)

        @pl.when(step + 1 < 2 * chips)
        def _():
            state_copy(step + 1, lax.rem(step + 1, 2)).start()

        state_copy(step, slot).wait()
        block = lax.rem(step, chips)
        for b in range(rows):
            for p in range(pairs):
                packed = jnp.concatenate([st_buf[slot, b, 2 * p], st_buf[slot, b, 2 * p + 1]], axis=1)
                target[block, b, p] = packed * decay[p]

    @pl.loop(0, chips)
    def _(step):
        weigh_step(step, p_out)

    pair_copy = remote(p_out, p_in, pair_sem.at[0], pair_sem.at[1], {"sp": chip * 2 + (1 - core)})
    pair_copy.start()

    @pl.loop(chips, 2 * chips)
    def _(step):
        weigh_step(step, acc)

    own_copies = [pltpu.make_async_copy(cache.at[pl.ds(me * rows, rows)], land.at[:, :, :, my_cols], own_sem.at[n])
                  for n, (cache, land) in enumerate(((k_in, k_land), (v_in, v_land)))]
    for copy in own_copies:
        copy.start()

    pair_copy.wait()

    @pl.loop(0, chips)
    def _(block):
        for b in range(rows):
            acc[block, b] = acc[block, b] + p_in[block, b]

    rs_copies = []
    for dc in (2, 1, 3):
        dst_chip = lax.rem(chip + dc, chips)
        rs_copies.append(remote(acc.at[dst_chip], rs_in.at[dc - 1], rs_sem.at[0, dc - 1], rs_sem.at[1, dc - 1], {"sp": dst_chip * 2 + core}))
    for copy in rs_copies:
        copy.start()
    start_round(1)

    def rms(vals):
        return vals * lax.rsqrt(jnp.mean(vals * vals, axis=-1, keepdims=True) + NORM_EPS)

    pad_rows = 8 - rows

    def pad8(vals):
        return jnp.concatenate([vals, jnp.zeros((pad_rows,) + vals.shape[1:], vals.dtype)], axis=0) if pad_rows else vals

    tokens = pad8(tok[...].astype(F32))
    normed = (rms(tokens) * lin_gain[...]).astype(BF16)
    weight_copies[0].wait()

    def act(n):
        lin = jnp.dot(normed, wv_qkv[n], preferred_element_type=F32)
        return (lin * jax.nn.sigmoid(lin)).astype(BF16).astype(F32)

    query, key, value = act(0), act(1), act(2)
    weight_copies[1].wait()
    gate = jax.nn.sigmoid(jnp.dot(normed, wv_gate[...], preferred_element_type=F32))
    query_t = jnp.transpose(query)
    key_t = jnp.transpose(key)
    o_s[...] = jnp.zeros_like(o_s)

    def column(cols, p, b):
        lo = cols[2 * p * head_dim:(2 * p + 1) * head_dim, b:b + 1]
        hi = cols[(2 * p + 1) * head_dim:(2 * p + 2) * head_dim, b:b + 1]
        return jnp.where(low_half, lo, hi)

    for copy in rs_copies:
        copy.wait()
    start_round(2)

    for p in range(pairs):
        lam = jnp.exp(-pair_slope(p))
        cols = slice(p * LANES, (p + 1) * LANES)
        for b in range(rows):
            moved = acc[chip, b, p] + rs_in[0, b, p] + rs_in[1, b, p] + rs_in[2, b, p]
            state = lam * moved + column(key_t, p, b) * value[b:b + 1, cols]
            o_s[b:b + 1, cols] = jnp.sum(column(query_t, p, b) * state, axis=0, keepdims=True)
            st_out[b, 2 * p] = state[:, :head_dim]
            st_out[b, 2 * p + 1] = state[:, head_dim:]

    def tp_sum(buf, vals, sems):
        buf[me_tp] = vals
        copies = []
        for dt in (2, 1, 3)[-(tp_size - 1):]:
            copies.append(remote(buf.at[me_tp], buf.at[me_tp], sems.at[0, dt - 1], sems.at[1, dt - 1], {"tp": lax.rem(me_tp + dt, tp_size)}))
        for copy in copies:
            copy.start()
        for copy in copies:
            copy.wait()
        total = buf[0]
        for n in range(1, tp_size):
            total = total + buf[n]
        return total

    lin_attn = o_s[...]
    squares = jnp.broadcast_to(jnp.sum(lin_attn * lin_attn, axis=-1, keepdims=True), (8, LANES))
    square_sum = tp_sum(sq_x, squares, sq_sem)[:, :1]
    mixed = (lin_attn * lax.rsqrt(square_sum / hidden_width + NORM_EPS) * out_gain[...] * gate).astype(BF16)
    weight_copies[2].wait()
    lin_out = tp_sum(y_x, jnp.dot(mixed, wv_lo[...], preferred_element_type=F32), y_sem)
    hidden = (normed.astype(F32) + lin_out).astype(BF16).astype(F32)
    normed_two = (rms(hidden) * attn_gain[...]).astype(BF16)

    weight_copies[3].wait()
    proj = lax.dot_general(normed_two, wv_in[...], NT, preferred_element_type=F32).astype(BF16).astype(F32)
    cols_in = proj.shape[1]
    quarter = head_dim // 4
    rotated = proj * rope[0:1, :] + pltpu.roll(proj, quarter, 1) * rope[1:2, :] + pltpu.roll(proj, cols_in - quarter, 1) * rope[2:3, :]
    rotated = rotated.astype(BF16).astype(F32)

    def segment_at(kv, segment):
        start = (kv * segments + segment) * head_dim
        block = rotated[:, start // LANES * LANES:start // LANES * LANES + LANES]
        if start % LANES != kv * head_dim:
            block = pltpu.roll(block, head_dim, 1)
        return jnp.where(low_half if kv == 0 else ~low_half, block, 0.0)

    for kv in range(kv_dev):
        key_rows, value_rows = segment_at(kv, group), segment_at(kv, group + 1)
        for i in range(group):
            row = (kv * group + i) * rows
            q_s[row:row + rows, :] = segment_at(kv, i)[:rows]
            kn_s[row:row + rows, :] = key_rows[:rows]
            vn_s[row:row + rows, :] = value_rows[:rows]

    q_x[me] = q_s[...].astype(BF16)
    q_copies = []
    for n, (dc, cr) in enumerate(peers):
        q_copies.append(remote(q_x.at[me], q_x.at[me], q_sem.at[0, n], q_sem.at[1, n], {"sp": peer_index(dc, cr)}))
    for copy in q_copies:
        copy.start()
    start_round(3)
    start_round(4)

    def shard_copies(j, slot):
        return [pltpu.make_async_copy(cache.at[pl.ds(j * rows, rows)], buf.at[slot], kb_sem.at[n, slot])
                for n, (cache, buf) in enumerate(((k_in, k_buf), (v_in, v_buf)))]

    for copy in shard_copies(0, 0):
        copy.start()

    rotated_t = jnp.transpose(rotated)
    lane16 = lax.broadcasted_iota(jnp.int32, (1, CACHE_EXTRA), 1)
    prompt_len = sp_size * shard_len
    for land, segment in ((k_land, group), (v_land, group + 1)):
        for kv in range(kv_dev):
            start = (kv * segments + segment) * head_dim
            for b in range(rows):
                tail = jnp.where(lane16 == 0, rotated_t[start:start + head_dim, b:b + 1], 0.0)
                land[b, kv, :, prompt_len:] = tail.astype(BF16)

    row_id = lax.broadcasted_iota(jnp.int32, (qrows, 1), 0)
    row_seq = lax.rem(row_id, rows)
    own_lanes = (row_id < group * rows) == low_half
    scale = head_dim ** -0.5
    stat_lane = lax.rem(lane, head_dim) < head_dim // 2

    for copy in q_copies:
        copy.wait()

    @pl.loop(0, sp_size)
    def _(j):
        slot = lax.rem(j, 2)

        @pl.when(j + 1 < sp_size)
        def _():
            for copy in shard_copies(j + 1, lax.rem(j + 1, 2)):
                copy.start()

        for copy in shard_copies(j, slot):
            copy.wait()
        queries = q_x[j]
        scores = jnp.zeros((qrows, shard_len), F32)
        for b in range(rows):
            keys = k_buf[slot, b].reshape(kv_dev * head_dim, shard_len)
            scores = jnp.where(row_seq == b, jnp.dot(queries, keys, preferred_element_type=F32), scores)
        scores = scores * scale
        peak = jnp.max(scores, axis=-1, keepdims=True)
        probs = jnp.exp(scores - peak)
        total = jnp.sum(probs, axis=-1, keepdims=True)
        probs = probs.astype(BF16)
        out = jnp.zeros((qrows, LANES), F32)
        for b in range(rows):
            vals = v_buf[slot, b].reshape(kv_dev * head_dim, shard_len)
            out = jnp.where(row_seq == b, lax.dot_general(probs, vals, NT, preferred_element_type=F32), out)
        pr_out[j] = jnp.where(own_lanes, out, jnp.where(stat_lane, peak, total))

    pr_copies = []
    for n, (dc, cr) in enumerate(peers):
        dst = peer_index(dc, cr)
        pr_copies.append(remote(pr_out.at[dst], pr_in.at[me], pr_sem.at[0, n], pr_sem.at[1, n], {"sp": dst}))
    for copy in pr_copies:
        copy.start()
    for round_idx in range(5, 2 * rows):
        start_round(round_idx)
    pr_in[me] = pr_out[me]

    new_score = jnp.sum(q_s[...] * kn_s[...], axis=-1, keepdims=True) * scale
    split = group * rows

    def stats(j, first):
        return jnp.concatenate([pr_in[j, :split, head_dim + first:head_dim + first + 1], pr_in[j, split:, first:first + 1]], axis=0)

    for copy in pr_copies:
        copy.wait()
    peaks = [stats(j, 0) for j in range(sp_size)]
    top = new_score
    for peak in peaks:
        top = jnp.maximum(top, peak)
    new_prob = jnp.exp(new_score - top)
    prob_sum = new_prob
    head = new_prob.astype(BF16).astype(F32) * vn_s[...]
    for j in range(sp_size):
        weight = jnp.exp(peaks[j] - top)
        prob_sum = prob_sum + weight * stats(j, head_dim // 2)
        head = head + weight * jnp.where(own_lanes, pr_in[j], 0.0)
    head = (head / prob_sum).astype(BF16).astype(F32)

    ho_s[...] = jnp.zeros_like(ho_s)
    for n in range(0, kv_dev * group, 2):
        block = None
        for m in (n, n + 1):
            kv = m // group
            piece = head[m * rows:(m + 1) * rows]
            if kv != m % 2:
                piece = pltpu.roll(piece, head_dim, 1)
            block = piece if block is None else block + piece
        ho_s[0:rows, n // 2 * LANES:(n // 2 + 1) * LANES] = block
    weight_copies[4].wait()
    attn_out = tp_sum(a_x, jnp.dot(ho_s[...].astype(BF16), wv_ao[...], preferred_element_type=F32), a_sem)
    hid_out[...] = (normed_two.astype(F32) + attn_out).astype(BF16)[:rows]

    for copy in own_copies:
        copy.wait()
    for copy in all_kv:
        copy.wait()


def put_kernel(*refs):
    count = (len(refs) - 1) // 2
    sems = refs[-1]
    copies = [pltpu.make_async_copy(refs[n], refs[count + n], sems.at[n]) for n in range(count)]
    for copy in copies:
        copy.start()
    for copy in copies:
        copy.wait()


def solution(mesh):
    sp_size = mesh.shape['sp']
    tp_size = mesh.shape['tp']
    chips = sp_size // 2

    def device_step(tokens, states, k_cache, v_cache, slopes, lin_gain, w_lin_qkv, w_lin_gate, out_gain, w_lin_out, attn_gain, w_attn_in, w_attn_out):
        rows, model = tokens.shape
        kv_dev, shard_len, head_dim = k_cache.shape[1:]
        heads = slopes.shape[0]
        segments = w_attn_in.shape[2]
        group = segments - 2
        width = heads * head_dim
        pairs = heads // 2
        cols_in = kv_dev * segments * head_dim
        qrows = kv_dev * group * rows
        prompt_len = sp_size * shard_len
        full_len = prompt_len + CACHE_EXTRA
        dims = (chips, tp_size, rows, heads, head_dim, kv_dev, group, shard_len)
        rope = jnp.asarray(rope_tables(kv_dev, segments, group, head_dim, prompt_len))

        vmem = pl.BlockSpec(memory_space=pltpu.VMEM)
        smem = pl.BlockSpec(memory_space=pltpu.SMEM)
        anym = pl.BlockSpec(memory_space=pl.ANY)
        dma = pltpu.SemaphoreType.DMA
        land_shape = (rows, kv_dev, head_dim, full_len)
        out_types = [((rows, model), BF16), ((rows, heads, head_dim, head_dim), F32), (land_shape, BF16), (land_shape, BF16)]
        scratch = [
            pltpu.VMEM((3, model, width), BF16),
            pltpu.VMEM((model, width), BF16),
            pltpu.VMEM((width, model), BF16),
            pltpu.VMEM((cols_in, model), BF16),
            pltpu.VMEM((width, model), BF16),
            pltpu.VMEM((2, rows, heads, head_dim, head_dim), F32),
            pltpu.VMEM((chips, rows, pairs, head_dim, LANES), F32),
            pltpu.VMEM((chips, rows, pairs, head_dim, LANES), F32),
            pltpu.VMEM((chips, rows, pairs, head_dim, LANES), F32),
            pltpu.VMEM((chips - 1, rows, pairs, head_dim, LANES), F32),
            pltpu.VMEM((tp_size, 8, LANES), F32),
            pltpu.VMEM((tp_size, 8, model), F32),
            pltpu.VMEM((tp_size, 8, model), F32),
            pltpu.VMEM((sp_size, qrows, LANES), BF16),
            pltpu.VMEM((sp_size, qrows, LANES), F32),
            pltpu.VMEM((sp_size, qrows, LANES), F32),
            pltpu.VMEM((2, rows, kv_dev, head_dim, shard_len), BF16),
            pltpu.VMEM((2, rows, kv_dev, head_dim, shard_len), BF16),
            pltpu.VMEM((8, width), F32),
            pltpu.VMEM((qrows, LANES), F32),
            pltpu.VMEM((qrows, LANES), F32),
            pltpu.VMEM((qrows, LANES), F32),
            pltpu.VMEM((8, width), F32),
            dma((5,)),
            dma((2,)),
            dma((2,)),
            dma((2, chips - 1)),
            dma((2, tp_size - 1)),
            dma((2, tp_size - 1)),
            dma((2, tp_size - 1)),
            dma((2, sp_size - 1)),
            dma((2, sp_size - 1)),
            dma((2 * rows, sp_size - 1)),
            dma((2 * rows, sp_size - 1)),
            dma((2,)),
            dma((2, 2)),
        ]
        landed = pl.pallas_call(
            functools.partial(step_kernel, dims),
            out_shape=[pltpu.VMEM(shape, dtype) for shape, dtype in out_types],
            in_specs=[vmem, smem, vmem, vmem, vmem, vmem] + [anym] * 8,
            out_specs=[vmem] * 4,
            scratch_shapes=scratch,
            compiler_params=pltpu.CompilerParams(collective_id=0, has_side_effects=True, vmem_limit_bytes=40 * 2 ** 20),
        )(
            tokens, slopes, lin_gain.reshape(1, -1), out_gain.reshape(1, -1), attn_gain.reshape(1, -1), rope,
            states, jnp.transpose(k_cache, (0, 1, 3, 2)), jnp.transpose(v_cache, (0, 1, 3, 2)),
            jnp.transpose(w_lin_qkv, (1, 0, 2)), w_lin_gate, w_lin_out,
            jnp.transpose(w_attn_in, (1, 2, 3, 0)).reshape(cols_in, model), w_attn_out,
        )
        hidden_out, state_new, k_out, v_out = pl.pallas_call(
            put_kernel,
            out_shape=[jax.ShapeDtypeStruct(shape, dtype) for shape, dtype in out_types],
            in_specs=[vmem] * 4,
            out_specs=[anym] * 4,
            scratch_shapes=[dma((4,))],
            compiler_params=pltpu.CompilerParams(vmem_limit_bytes=2 * 2 ** 20),
        )(*landed)
        return hidden_out, state_new, jnp.transpose(k_out, (0, 1, 3, 2)), jnp.transpose(v_out, (0, 1, 3, 2))

    batch_spec = P(('dp', 'sp'), None)
    head_spec = P(('dp', 'sp'), 'tp', None, None)
    cache_spec = P('dp', 'tp', 'sp', None)
    in_specs = (batch_spec, P('sp', 'dp', 'tp', None, None), cache_spec, cache_spec, P('tp'), P(None), P(None, None, 'tp'), P(None, 'tp'), P('tp'), P('tp', None), P(None), P(None, 'tp', None, None), P('tp', None))
    out_specs = (batch_spec, head_spec, head_spec, head_spec)
    return jax.shard_map(device_step, mesh=mesh, in_specs=in_specs, out_specs=out_specs, check_vma=False)
```

time: 373 us -> 223 us (0.60)
  the two profiles are of different devices: /device:TPU:96 before, /device:TPU:97 now
where the time goes in v1:
time: 223 us
  Pallas kernels  222 us (100%)
    pallas_call x1, Pallas kernels, device_step(): pl.pallas_call(functools.partial(step_kernel, dims), out_shape=[pltpu.VME...  216 us
    pallas_call x1, Pallas kernels, device_step(): pl.pallas_call(put_kernel, out_shape=[jax.ShapeDtypeStruct(shape, dtype)...  6.63 us

profile of v1, /device:TPU:97, one launch (start us, length us, event | category | flops | bytes accessed | tf_op | source)
XLA Modules:
  0.0 223.1 jit_solution(1935937058212071073)
XLA Ops:
  0.6 215.8 %shard_map.165 = (bf16[4,2048]{1,0:T(4,128)(2,1)S(1)}, f32[4,8,64,64]{3,2,1,0:T(8,128)S(1)}, bf16[4,2,64,8208]{3,2,1,0:T(8,128)(2,1)S(1)}, bf16[4,2,64,8208]{3,2,1,0:T(8,128)(2,1)S(1)}) custom-call(bf16[4,2048]{1,0:T(4,128)(2,1)} %tok.1, f32[8]{0:T(128)} %slopes.1, f32[1,2048]{1,0:T(1,128)} %bitcast.15, f32[1,512]{1,0:T(1,128)} %bitcast.17, ...), custom_call_target="tpu_custom_call" | custom-call | tf_op jit(solution)/shard_map/pallas_call | solution.py:431
  216.4 6.6 %shard_map.166 = (bf16[4,2048]{1,0:T(4,128)(2,1)}, f32[4,8,64,64]{3,2,1,0:T(8,128)}, bf16[4,2,64,8208]{3,2,1,0:T(8,128)(2,1)}, bf16[4,2,64,8208]{3,2,1,0:T(8,128)(2,1)}) custom-call(bf16[4,2048]{1,0:T(4,128)(2,1)S(1)} %get-tuple-element.12.refs_0_, f32[4,8,64,64]{3,2,1,0:T(8,128)S(1)} %get-tuple-element.13.refs_1_, ...), custom_call_target="tpu_custom_call" | custom-call | tf_op jit(solution)/shard_map/pallas_call | solution.py:444

commit v2 on v1

--- a/solution.py
+++ b/solution.py
@@ -35,16 +35,16 @@
     return table.reshape(8, kv_dev * segments * head_dim)
 
 
-def step_kernel(dims, tok, slopes, lin_gain, out_gain, attn_gain, rope, states, k_in, v_in, w_qkv, w_gate, w_lo, w_in, w_ao,
+def step_kernel(dims, tok_in, slopes, lin_gain_in, out_gain_in, attn_gain_in, rope_in, states, k_in, v_in, w_qkv, w_gate, w_lo, w_in, w_ao,
                 hid_out, st_out, k_land, v_land,
-                wv_qkv, wv_gate, wv_lo, wv_in, wv_ao, st_buf, p_out, p_in, acc, rs_in, sq_x, y_x, a_x, q_x, pr_out, pr_in,
+                tok, lin_gain, out_gain, attn_gain, rope, wv_qkv, wv_gate, wv_lo, wv_in, wv_ao, st_buf, p_out, p_in, acc, relay_in, rs_in, sq_x, y_x, a_x, q_x, pr_out, pr_in,
                 k_buf, v_buf, o_s, q_s, kn_s, vn_s, ho_s,
-                w_sem, st_sem, pair_sem, rs_sem, sq_sem, y_sem, a_sem, q_sem, pr_sem, kv_send, kv_recv, own_sem, kb_sem):
+                in_sem, w_sem, st_sem, pair_sem, rs_sem, sq_sem, y_sem, a_sem, q_sem, pr_sem, kv_send, kv_recv, own_sem, kb_sem):
     chips, tp_size, rows, heads, head_dim, kv_dev, group, shard_len = dims
     sp_size = 2 * chips
     pairs = heads // 2
     width = heads * head_dim
-    model = tok.shape[1]
+    model = tok_in.shape[1]
     hidden_width = tp_size * width
     segments = group + 2
     qrows = kv_dev * group * rows
@@ -95,6 +95,10 @@
         return pltpu.make_async_copy(states.at[0, pl.ds(dest * rows, rows)], st_buf.at[slot], st_sem.at[slot])
 
     state_copy(0, 0).start()
+    small_copies = [pltpu.make_async_copy(src, dst, in_sem.at[n]) for n, (src, dst) in enumerate(
+        ((tok_in, tok), (lin_gain_in, lin_gain), (out_gain_in, out_gain), (attn_gain_in, attn_gain), (rope_in, rope)))]
+    for copy in small_copies:
+        copy.start()
     weight_copies = [pltpu.make_async_copy(src, dst, w_sem.at[n]) for n, (src, dst) in enumerate(
         ((w_qkv, wv_qkv), (w_gate, wv_gate), (w_lo, wv_lo), (w_in, wv_in), (w_ao, wv_ao)))]
     for copy in weight_copies:
@@ -146,11 +150,17 @@
         for b in range(rows):
             acc[block, b] = acc[block, b] + p_in[block, b]
 
-    rs_copies = []
-    for dc in (2, 1, 3):
-        dst_chip = lax.rem(chip + dc, chips)
-        rs_copies.append(remote(acc.at[dst_chip], rs_in.at[dc - 1], rs_sem.at[0, dc - 1], rs_sem.at[1, dc - 1], {"sp": dst_chip * 2 + core}))
-    for copy in rs_copies:
+    nexts = [(lax.rem(chip + dc, chips), {"sp": lax.rem(chip + dc, chips) * 2 + core}) for dc in (1, chips - 1)]
+    far = lax.rem(chip + 2, chips)
+    half = rows // 2
+    parts = [pl.ds(0, half), pl.ds(half, half)]
+
+    def rs_copy(n, src, dst, side):
+        return remote(src, dst, rs_sem.at[0, n], rs_sem.at[1, n], nexts[side][1])
+
+    relay_copies = [rs_copy(side, acc.at[far, parts[side]], relay_in.at[side], side) for side in range(2)]
+    rs_copies = [rs_copy(2 + side, acc.at[nexts[side][0], parts[1 - side]], rs_in.at[side, parts[1 - side]], side) for side in range(2)]
+    for copy in relay_copies + rs_copies:
         copy.start()
     start_round(1)
 
@@ -162,6 +172,8 @@
     def pad8(vals):
         return jnp.concatenate([vals, jnp.zeros((pad_rows,) + vals.shape[1:], vals.dtype)], axis=0) if pad_rows else vals
 
+    for copy in small_copies:
+        copy.wait()
     tokens = pad8(tok[...].astype(F32))
     normed = (rms(tokens) * lin_gain[...]).astype(BF16)
     weight_copies[0].wait()
@@ -175,6 +187,15 @@
     gate = jax.nn.sigmoid(jnp.dot(normed, wv_gate[...], preferred_element_type=F32))
     query_t = jnp.transpose(query)
     key_t = jnp.transpose(key)
+    for side in range(2):
+        relay_copies[side].wait()
+        block = nexts[side][0]
+        for b in range(half):
+            acc[block, side * half + b] = acc[block, side * half + b] + relay_in[side, b]
+        copy = rs_copy(4 + side, acc.at[block, parts[side]], rs_in.at[side, parts[side]], side)
+        copy.start()
+        rs_copies.append(copy)
+    start_round(2)
     o_s[...] = jnp.zeros_like(o_s)
 
     def column(cols, p, b):
@@ -184,13 +205,12 @@
 
     for copy in rs_copies:
         copy.wait()
-    start_round(2)
 
     for p in range(pairs):
         lam = jnp.exp(-pair_slope(p))
         cols = slice(p * LANES, (p + 1) * LANES)
         for b in range(rows):
-            moved = acc[chip, b, p] + rs_in[0, b, p] + rs_in[1, b, p] + rs_in[2, b, p]
+            moved = acc[chip, b, p] + rs_in[0, b, p] + rs_in[1, b, p]
             state = lam * moved + column(key_t, p, b) * value[b:b + 1, cols]
             o_s[b:b + 1, cols] = jnp.sum(column(query_t, p, b) * state, axis=0, keepdims=True)
             st_out[b, 2 * p] = state[:, :head_dim]
@@ -357,7 +377,12 @@
 def put_kernel(*refs):
     count = (len(refs) - 1) // 2
     sems = refs[-1]
-    copies = [pltpu.make_async_copy(refs[n], refs[count + n], sems.at[n]) for n in range(count)]
+    copies = []
+    for n in (2, 3, 1, 0):
+        pieces = refs[n].shape[0] if n > 0 else 1
+        for i in range(pieces):
+            src, dst = (refs[n].at[i], refs[count + n].at[i]) if pieces > 1 else (refs[n], refs[count + n])
+            copies.append(pltpu.make_async_copy(src, dst, sems.at[len(copies)]))
     for copy in copies:
         copy.start()
     for copy in copies:
@@ -391,6 +416,11 @@
         land_shape = (rows, kv_dev, head_dim, full_len)
         out_types = [((rows, model), BF16), ((rows, heads, head_dim, head_dim), F32), (land_shape, BF16), (land_shape, BF16)]
         scratch = [
+            pltpu.VMEM((rows, model), BF16),
+            pltpu.VMEM((1, model), F32),
+            pltpu.VMEM((1, width), F32),
+            pltpu.VMEM((1, model), F32),
+            pltpu.VMEM((8, cols_in), F32),
             pltpu.VMEM((3, model, width), BF16),
             pltpu.VMEM((model, width), BF16),
             pltpu.VMEM((width, model), BF16),
@@ -400,7 +430,8 @@
             pltpu.VMEM((chips, rows, pairs, head_dim, LANES), F32),
             pltpu.VMEM((chips, rows, pairs, head_dim, LANES), F32),
             pltpu.VMEM((chips, rows, pairs, head_dim, LANES), F32),
-            pltpu.VMEM((chips - 1, rows, pairs, head_dim, LANES), F32),
+            pltpu.VMEM((2, rows // 2, pairs, head_dim, LANES), F32),
+            pltpu.VMEM((2, rows, pairs, head_dim, LANES), F32),
             pltpu.VMEM((tp_size, 8, LANES), F32),
             pltpu.VMEM((tp_size, 8, model), F32),
             pltpu.VMEM((tp_size, 8, model), F32),
@@ -415,9 +446,10 @@
             pltpu.VMEM((qrows, LANES), F32),
             pltpu.VMEM((8, width), F32),
             dma((5,)),
+            dma((5,)),
             dma((2,)),
             dma((2,)),
-            dma((2, chips - 1)),
+            dma((2, 6)),
             dma((2, tp_size - 1)),
             dma((2, tp_size - 1)),
             dma((2, tp_size - 1)),
@@ -431,7 +463,7 @@
         landed = pl.pallas_call(
             functools.partial(step_kernel, dims),
             out_shape=[pltpu.VMEM(shape, dtype) for shape, dtype in out_types],
-            in_specs=[vmem, smem, vmem, vmem, vmem, vmem] + [anym] * 8,
+            in_specs=[anym, smem, anym, anym, anym, anym] + [anym] * 8,
             out_specs=[vmem] * 4,
             scratch_shapes=scratch,
             compiler_params=pltpu.CompilerParams(collective_id=0, has_side_effects=True, vmem_limit_bytes=40 * 2 ** 20),
@@ -446,7 +478,7 @@
             out_shape=[jax.ShapeDtypeStruct(shape, dtype) for shape, dtype in out_types],
             in_specs=[vmem] * 4,
             out_specs=[anym] * 4,
-            scratch_shapes=[dma((4,))],
+            scratch_shapes=[dma((3 * rows + 1,))],
             compiler_params=pltpu.CompilerParams(vmem_limit_bytes=2 * 2 ** 20),
         )(*landed)
         return hidden_out, state_new, jnp.transpose(k_out, (0, 1, 3, 2)), jnp.transpose(v_out, (0, 1, 3, 2))

time: 223 us -> 217 us (0.973)
  Pallas kernels: 222 us -> 216 us
    pallas_call x1, Pallas kernels: 216 us -> 210 us  [device_step(): pl.pallas_call(functools.partial(step_kernel, dims), out_shape=[pltpu.VME...]
where the time goes in v2:
time: 217 us
  Pallas kernels  216 us (100%)
    pallas_call x1, Pallas kernels, device_step(): pl.pallas_call(functools.partial(step_kernel, dims), out_shape=[pltpu.VME...  210 us
    pallas_call x1, Pallas kernels, device_step(): pl.pallas_call(put_kernel, out_shape=[jax.ShapeDtypeStruct(shape, dtype)...  6.3 us

profile of v2, /device:TPU:97, one launch (start us, length us, event | category | flops | bytes accessed | tf_op | source)
XLA Modules:
  0.0 217.1 jit_solution(17727480048207610566)
XLA Ops:
  0.6 210.1 %shard_map.165 = (bf16[4,2048]{1,0:T(4,128)(2,1)S(1)}, f32[4,8,64,64]{3,2,1,0:T(8,128)S(1)}, bf16[4,2,64,8208]{3,2,1,0:T(8,128)(2,1)S(1)}, bf16[4,2,64,8208]{3,2,1,0:T(8,128)(2,1)S(1)}) custom-call(bf16[4,2048]{1,0:T(4,128)(2,1)} %tok_in.1, f32[8]{0:T(128)} %slopes.1, f32[1,2048]{1,0:T(1,128)} %bitcast.15, f32[1,512]{1,0:T(1,128)} %bitcast.17, ...), custom_call_target="tpu_custom_call" | custom-call | tf_op jit(solution)/shard_map/pallas_call | solution.py:463
  210.8 6.3 %shard_map.166 = (bf16[4,2048]{1,0:T(4,128)(2,1)}, f32[4,8,64,64]{3,2,1,0:T(8,128)}, bf16[4,2,64,8208]{3,2,1,0:T(8,128)(2,1)}, bf16[4,2,64,8208]{3,2,1,0:T(8,128)(2,1)}) custom-call(bf16[4,2048]{1,0:T(4,128)(2,1)S(1)} %get-tuple-element.12.refs_0_, f32[4,8,64,64]{3,2,1,0:T(8,128)S(1)} %get-tuple-element.13.refs_1_, ...), custom_call_target="tpu_custom_call" | custom-call | tf_op jit(solution)/shard_map/pallas_call | solution.py:476

commit v3 on v2

--- a/solution.py
+++ b/solution.py
@@ -39,7 +39,7 @@
                 hid_out, st_out, k_land, v_land,
                 tok, lin_gain, out_gain, attn_gain, rope, wv_qkv, wv_gate, wv_lo, wv_in, wv_ao, st_buf, p_out, p_in, acc, relay_in, rs_in, sq_x, y_x, a_x, q_x, pr_out, pr_in,
                 k_buf, v_buf, o_s, q_s, kn_s, vn_s, ho_s,
-                in_sem, w_sem, st_sem, pair_sem, rs_sem, sq_sem, y_sem, a_sem, q_sem, pr_sem, kv_send, kv_recv, own_sem, kb_sem):
+                go_sem, in_sem, w_sem, st_sem, pair_sem, rs_sem, sq_sem, y_sem, a_sem, q_sem, pr_sem, kv_send, kv_recv, own_sem, kb_sem):
     chips, tp_size, rows, heads, head_dim, kv_dev, group, shard_len = dims
     sp_size = 2 * chips
     pairs = heads // 2
@@ -61,9 +61,28 @@
     barrier = pltpu.get_barrier_semaphore()
     for dc, cr in peers:
         pl.semaphore_signal(barrier, inc=1, device_id={"sp": peer_index(dc, cr)}, device_id_type=MESH)
-    for dt in range(1, tp_size):
-        pl.semaphore_signal(barrier, inc=1, device_id={"tp": lax.rem(me_tp + dt, tp_size)}, device_id_type=MESH)
-    pl.semaphore_wait(barrier, len(peers) + tp_size - 1)
+
+    @pl.when(me_tp == 0)
+    def _():
+        pl.semaphore_wait(barrier, len(peers))
+        for other in range(1, tp_size):
+            pl.semaphore_signal(barrier, inc=1, device_id={"tp": other}, device_id_type=MESH)
+
+    @pl.when(me_tp != 0)
+    def _():
+        pl.semaphore_wait(barrier, len(peers) + 1)
+        pl.semaphore_signal(barrier, inc=1, device_id={"tp": 0}, device_id_type=MESH)
+
+    def wait_for_tp():
+        @pl.when(me_tp == 0)
+        def _():
+            pl.semaphore_wait(barrier, tp_size - 1)
+            for other in range(1, tp_size):
+                pl.semaphore_signal(go_sem, inc=1, device_id={"tp": other}, device_id_type=MESH)
+
+        @pl.when(me_tp != 0)
+        def _():
+            pl.semaphore_wait(go_sem, 1)
 
     def remote(src, dst, send, recv, device):
         return pltpu.make_async_remote_copy(src_ref=src, dst_ref=dst, send_sem=send, recv_sem=recv, device_id=device, device_id_type=MESH)
@@ -230,6 +249,7 @@
             total = total + buf[n]
         return total
 
+    wait_for_tp()
     lin_attn = o_s[...]
     squares = jnp.broadcast_to(jnp.sum(lin_attn * lin_attn, axis=-1, keepdims=True), (8, LANES))
     square_sum = tp_sum(sq_x, squares, sq_sem)[:, :1]
@@ -253,13 +273,17 @@
             block = pltpu.roll(block, head_dim, 1)
         return jnp.where(low_half if kv == 0 else ~low_half, block, 0.0)
 
-    for kv in range(kv_dev):
-        key_rows, value_rows = segment_at(kv, group), segment_at(kv, group + 1)
-        for i in range(group):
-            row = (kv * group + i) * rows
-            q_s[row:row + rows, :] = segment_at(kv, i)[:rows]
-            kn_s[row:row + rows, :] = key_rows[:rows]
-            vn_s[row:row + rows, :] = value_rows[:rows]
+    def packed_at(segment):
+        return (segment_at(0, segment) + segment_at(1, segment))[:rows]
+
+    key_rows, value_rows = packed_at(group), packed_at(group + 1)
+    for i in range(group):
+        q_s[i * rows:(i + 1) * rows, :] = packed_at(i)
+        kn_s[i * rows:(i + 1) * rows, :] = key_rows
+        vn_s[i * rows:(i + 1) * rows, :] = value_rows
+
+    def spread(vals):
+        return jnp.concatenate([jnp.where(low_half, vals, 0.0), jnp.where(low_half, 0.0, vals)], axis=0)
 
     q_x[me] = q_s[...].astype(BF16)
     q_copies = []
@@ -289,9 +313,8 @@
 
     row_id = lax.broadcasted_iota(jnp.int32, (qrows, 1), 0)
     row_seq = lax.rem(row_id, rows)
-    own_lanes = (row_id < group * rows) == low_half
+    split = group * rows
     scale = head_dim ** -0.5
-    stat_lane = lax.rem(lane, head_dim) < head_dim // 2
 
     for copy in q_copies:
         copy.wait()
@@ -307,7 +330,7 @@
 
         for copy in shard_copies(j, slot):
             copy.wait()
-        queries = q_x[j]
+        queries = spread(q_x[j].astype(F32)).astype(BF16)
         scores = jnp.zeros((qrows, shard_len), F32)
         for b in range(rows):
             keys = k_buf[slot, b].reshape(kv_dev * head_dim, shard_len)
@@ -321,7 +344,10 @@
         for b in range(rows):
             vals = v_buf[slot, b].reshape(kv_dev * head_dim, shard_len)
             out = jnp.where(row_seq == b, lax.dot_general(probs, vals, NT, preferred_element_type=F32), out)
-        pr_out[j] = jnp.where(own_lanes, out, jnp.where(stat_lane, peak, total))
+        pr_out[j, :split] = jnp.where(low_half, out[:split], out[split:])
+        stats = jnp.transpose(jnp.where(low_half, peak, total))
+        stats = jnp.concatenate([stats[:4], stats[head_dim:head_dim + 4]], axis=0)
+        pr_out[j, split:] = jnp.concatenate([stats, jnp.zeros((8, LANES - qrows), F32)], axis=1)
 
     pr_copies = []
     for n, (dc, cr) in enumerate(peers):
@@ -333,25 +359,22 @@
         start_round(round_idx)
     pr_in[me] = pr_out[me]
 
-    new_score = jnp.sum(q_s[...] * kn_s[...], axis=-1, keepdims=True) * scale
-    split = group * rows
-
-    def stats(j, first):
-        return jnp.concatenate([pr_in[j, :split, head_dim + first:head_dim + first + 1], pr_in[j, split:, first:first + 1]], axis=0)
+    new_score = jnp.sum(spread(q_s[...] * kn_s[...]), axis=-1, keepdims=True) * scale
 
     for copy in pr_copies:
         copy.wait()
-    peaks = [stats(j, 0) for j in range(sp_size)]
+    stats = [jnp.transpose(pr_in[j, split:]) for j in range(sp_size)]
+    peaks = [stat[:qrows, 0:1] for stat in stats]
     top = new_score
     for peak in peaks:
         top = jnp.maximum(top, peak)
     new_prob = jnp.exp(new_score - top)
     prob_sum = new_prob
-    head = new_prob.astype(BF16).astype(F32) * vn_s[...]
+    head = new_prob.astype(BF16).astype(F32) * spread(vn_s[...])
     for j in range(sp_size):
         weight = jnp.exp(peaks[j] - top)
-        prob_sum = prob_sum + weight * stats(j, head_dim // 2)
-        head = head + weight * jnp.where(own_lanes, pr_in[j], 0.0)
+        prob_sum = prob_sum + weight * stats[j][:qrows, 4:5]
+        head = head + weight * spread(pr_in[j, :split])
     head = (head / prob_sum).astype(BF16).astype(F32)
 
     ho_s[...] = jnp.zeros_like(ho_s)
@@ -435,16 +458,17 @@
             pltpu.VMEM((tp_size, 8, LANES), F32),
             pltpu.VMEM((tp_size, 8, model), F32),
             pltpu.VMEM((tp_size, 8, model), F32),
-            pltpu.VMEM((sp_size, qrows, LANES), BF16),
-            pltpu.VMEM((sp_size, qrows, LANES), F32),
-            pltpu.VMEM((sp_size, qrows, LANES), F32),
+            pltpu.VMEM((sp_size, group * rows, LANES), BF16),
+            pltpu.VMEM((sp_size, group * rows + 8, LANES), F32),
+            pltpu.VMEM((sp_size, group * rows + 8, LANES), F32),
             pltpu.VMEM((2, rows, kv_dev, head_dim, shard_len), BF16),
             pltpu.VMEM((2, rows, kv_dev, head_dim, shard_len), BF16),
             pltpu.VMEM((8, width), F32),
-            pltpu.VMEM((qrows, LANES), F32),
-            pltpu.VMEM((qrows, LANES), F32),
-            pltpu.VMEM((qrows, LANES), F32),
+            pltpu.VMEM((group * rows, LANES), F32),
+            pltpu.VMEM((group * rows, LANES), F32),
+            pltpu.VMEM((group * rows, LANES), F32),
             pltpu.VMEM((8, width), F32),
+            pltpu.SemaphoreType.REGULAR,
             dma((5,)),
             dma((5,)),
             dma((2,)),

time: 217 us -> 214 us (0.986)
  Pallas kernels: 216 us -> 213 us
    pallas_call x1, Pallas kernels: 210 us -> 206 us  [device_step(): pl.pallas_call(functools.partial(step_kernel, dims), out_shape=[pltpu.VME...]
where the time goes in v3:
time: 214 us; the launch traced here: 213 us
  Pallas kernels  213 us (100%)
    pallas_call x1, Pallas kernels, device_step(): pl.pallas_call(functools.partial(step_kernel, dims), out_shape=[pltpu.VME...  206 us
    pallas_call x1, Pallas kernels, device_step(): pl.pallas_call(put_kernel, out_shape=[jax.ShapeDtypeStruct(shape, dtype)...  6.3 us

profile of v3, /device:TPU:97, one launch (start us, length us, event | category | flops | bytes accessed | tf_op | source)
XLA Modules:
  0.0 213.4 jit_solution(18085704846344592734)
XLA Ops:
  0.6 206.5 %shard_map.165 = (bf16[4,2048]{1,0:T(4,128)(2,1)S(1)}, f32[4,8,64,64]{3,2,1,0:T(8,128)S(1)}, bf16[4,2,64,8208]{3,2,1,0:T(8,128)(2,1)S(1)}, bf16[4,2,64,8208]{3,2,1,0:T(8,128)(2,1)S(1)}) custom-call(bf16[4,2048]{1,0:T(4,128)(2,1)} %tok_in.1, f32[8]{0:T(128)} %slopes.1, f32[1,2048]{1,0:T(1,128)} %bitcast.15, f32[1,512]{1,0:T(1,128)} %bitcast.17, ...), custom_call_target="tpu_custom_call" | custom-call | tf_op jit(solution)/shard_map/pallas_call | solution.py:487
  207.1 6.3 %shard_map.166 = (bf16[4,2048]{1,0:T(4,128)(2,1)}, f32[4,8,64,64]{3,2,1,0:T(8,128)}, bf16[4,2,64,8208]{3,2,1,0:T(8,128)(2,1)}, bf16[4,2,64,8208]{3,2,1,0:T(8,128)(2,1)}) custom-call(bf16[4,2048]{1,0:T(4,128)(2,1)S(1)} %get-tuple-element.12.refs_0_, f32[4,8,64,64]{3,2,1,0:T(8,128)S(1)} %get-tuple-element.13.refs_1_, ...), custom_call_target="tpu_custom_call" | custom-call | tf_op jit(solution)/shard_map/pallas_call | solution.py:500

commit v4 on v0

v4 whole, which is shorter than its diff:
```python
import functools

import numpy as np

import jax
import jax.numpy as jnp
from jax import lax
from jax.experimental import pallas as pl
from jax.experimental.pallas import tpu as pltpu
from jax.sharding import PartitionSpec as P

NORM_EPS = 1e-6
ROPE_BASE = 10000000.0
CACHE_EXTRA = 16
LANES = 128
F32 = jnp.float32
BF16 = jnp.bfloat16
MESH = pl.DeviceIdType.MESH
NT = (((1,), (1,)), ((), ()))


def rope_tables(kv_dev, segments, group, head_dim, position):
    rope_dim = head_dim // 2
    half = rope_dim // 2
    exponents = -np.arange(0, rope_dim, 2, dtype=np.float32) / np.float32(rope_dim)
    angles = (np.float32(position) * np.float32(ROPE_BASE) ** exponents).astype(np.float32)
    cosine, sine = np.cos(angles), np.sin(angles)
    table = np.zeros((8, kv_dev, segments, head_dim), np.float32)
    table[0] = 1.0
    for segment in range(group + 1):
        table[0, :, segment, :half] = cosine
        table[0, :, segment, half:rope_dim] = cosine
        table[1, :, segment, half:rope_dim] = sine
        table[2, :, segment, :half] = -sine
    return table.reshape(8, kv_dev * segments * head_dim)


def step_kernel(dims, tok_in, slopes_in, lin_gain_in, out_gain_in, attn_gain_in, rope_in, states, k_in, v_in, w_qkv, w_gate, w_lo, w_in, w_ao,
                hid_out, st_out, k_land, v_land,
                slopes, tok, lin_gain, out_gain, attn_gain, rope, wv_qkv, wv_gate, wv_lo, wv_in, wv_ao, st_buf, p_out, p_in, acc, relay_in, rs_in, sq_x, y_x, a_x, q_x, pr_out, pr_pair, pr_mine, pr_in,
                k_buf, v_buf, o_s, q_s, kn_s, vn_s, ho_s,
                go_sem, pair_sem, rs_sem, sq_sem, y_sem, a_sem, q_sem, pr_sem, kv_send, kv_recv):
    chips, tp_size, rows, heads, head_dim, kv_dev, group, shard_len = dims
    sp_size = 2 * chips
    pairs = heads // 2
    width = heads * head_dim
    model = tok_in.shape[1]
    hidden_width = tp_size * width
    segments = group + 2
    qrows = kv_dev * group * rows

    me = lax.axis_index("sp")
    me_tp = lax.axis_index("tp")
    chip = me // 2
    core = lax.rem(me, 2)
    peers = [(dc, cr) for dc, cr in ((2, 0), (1, 0), (3, 0), (2, 1), (1, 1), (3, 1), (0, 1))]

    def peer_index(dc, cr):
        return lax.rem(chip + dc, chips) * 2 + (core if cr == 0 else 1 - core)

    barrier = pltpu.get_barrier_semaphore()
    for dc, cr in peers:
        pl.semaphore_signal(barrier, inc=1, device_id={"sp": peer_index(dc, cr)}, device_id_type=MESH)

    @pl.when(me_tp == 0)
    def _():
        pl.semaphore_wait(barrier, len(peers))
        for other in range(1, tp_size):
            pl.semaphore_signal(barrier, inc=1, device_id={"tp": other}, device_id_type=MESH)

    @pl.when(me_tp != 0)
    def _():
        pl.semaphore_wait(barrier, len(peers) + 1)
        pl.semaphore_signal(barrier, inc=1, device_id={"tp": 0}, device_id_type=MESH)

    def wait_for_tp():
        @pl.when(me_tp == 0)
        def _():
            pl.semaphore_wait(barrier, tp_size - 1)
            for other in range(1, tp_size):
                pl.semaphore_signal(go_sem, inc=1, device_id={"tp": other}, device_id_type=MESH)

        @pl.when(me_tp != 0)
        def _():
            pl.semaphore_wait(go_sem, 1)

    def remote(src, dst, send, recv, device):
        return pltpu.make_async_remote_copy(src_ref=src, dst_ref=dst, send_sem=send, recv_sem=recv, device_id=device, device_id_type=MESH)

    partner = {"sp": chip * 2 + (1 - core)}
    my_cols = pl.ds(pl.multiple_of(me * shard_len, LANES), shard_len)

    def kv_copies(round_idx):
        cache, land = ((k_in, k_land), (v_in, v_land))[round_idx % 2]
        row = round_idx // 2
        copies = []
        for n, (dc, cr) in enumerate(peers):
            dst = peer_index(dc, cr)
            copies.append(remote(cache.at[dst * rows + row], land.at[row, :, :, my_cols], kv_send.at[round_idx % 2], kv_recv.at[round_idx % 2], {"sp": dst}))
        return copies

    def start_round(round_idx):
        for copy in kv_copies(round_idx):
            copy.start()

    def total_of(ref, sems):
        return remote(ref, ref, sems[0], sems[1], partner)

    start_round(0)

    def decode_step(in_sem, w_sem, st_sem, own_sem, kb_sem):
        def state_copy(step, slot):
            target_core = jnp.where(step < chips, 1 - core, core)
            dest = lax.rem(step, chips) * 2 + target_core
            return pltpu.make_async_copy(states.at[0, pl.ds(dest * rows, rows)], st_buf.at[slot], st_sem.at[slot])

        slope_copy = pltpu.make_async_copy(slopes_in, slopes, in_sem.at[5])
        slope_copy.start()
        state_copy(0, 0).start()
        small_copies = [pltpu.make_async_copy(src, dst, in_sem.at[n]) for n, (src, dst) in enumerate(
            ((tok_in, tok), (lin_gain_in, lin_gain), (out_gain_in, out_gain), (attn_gain_in, attn_gain), (rope_in, rope)))]
        for copy in small_copies:
            copy.start()
        weight_copies = [pltpu.make_async_copy(src, dst, w_sem.at[n]) for n, (src, dst) in enumerate(
            ((w_qkv, wv_qkv), (w_gate, wv_gate), (w_lo, wv_lo), (w_in, wv_in), (w_ao, wv_ao)))]
        for copy in weight_copies:
            copy.start()

        lane = lax.broadcasted_iota(jnp.int32, (1, LANES), 1)
        low_half = lane < head_dim

        def pair_slope(p):
            return jnp.where(low_half, jnp.full((1, LANES), slopes[2 * p], F32), jnp.full((1, LANES), slopes[2 * p + 1], F32))

        slope_copy.wait()
        offset = (shard_len * (sp_size - 1 - me)).astype(F32)
        decay = [jnp.exp(-pair_slope(p) * offset) for p in range(pairs)]

        def weigh_step(step, target):
            slot = lax.rem(step, 2)

            @pl.when(step + 1 < 2 * chips)
            def _():
                state_copy(step + 1, lax.rem(step + 1, 2)).start()

            state_copy(step, slot).wait()
            block = lax.rem(step, chips)
            for b in range(rows):
                for p in range(pairs):
                    packed = jnp.concatenate([st_buf[slot, b, 2 * p], st_buf[slot, b, 2 * p + 1]], axis=1)
                    target[block, b, p] = packed * decay[p]

        @pl.loop(0, chips)
        def _(step):
            weigh_step(step, p_out)

        pair_copy = remote(p_out, p_in, pair_sem.at[0], pair_sem.at[1], partner)
        pair_copy.start()

        @pl.loop(chips, 2 * chips)
        def _(step):
            weigh_step(step, acc)

        own_copies = [pltpu.make_async_copy(cache.at[pl.ds(me * rows, rows)], land.at[:, :, :, my_cols], own_sem.at[n])
                      for n, (cache, land) in enumerate(((k_in, k_land), (v_in, v_land)))]
        for copy in own_copies:
            copy.start()

        pair_copy.wait()

        @pl.loop(0, chips)
        def _(block):
            for b in range(rows):
                acc[block, b] = acc[block, b] + p_in[block, b]

        nexts = [(lax.rem(chip + dc, chips), {"sp": lax.rem(chip + dc, chips) * 2 + core}) for dc in (1, chips - 1)]
        far = lax.rem(chip + 2, chips)
        half = rows // 2
        parts = [pl.ds(0, half), pl.ds(half, half)]

        def rs_copy(n, src, dst, side):
            return remote(src, dst, rs_sem.at[n], rs_sem.at[n + 1], nexts[side][1])

        relay_copies = [rs_copy(0, acc.at[far, parts[side]], relay_in.at[side], side) for side in range(2)]
        rs_copies = [rs_copy(2, acc.at[nexts[side][0], parts[1 - side]], rs_in.at[side, parts[1 - side]], side) for side in range(2)]
        for copy in relay_copies + rs_copies:
            copy.start()
        start_round(1)

        def rms(vals):
            return vals * lax.rsqrt(jnp.mean(vals * vals, axis=-1, keepdims=True) + NORM_EPS)

        pad_rows = 8 - rows

        def pad8(vals):
            return jnp.concatenate([vals, jnp.zeros((pad_rows,) + vals.shape[1:], vals.dtype)], axis=0) if pad_rows else vals

        for copy in small_copies:
            copy.wait()
        tokens = pad8(tok[...].astype(F32))
        normed = (rms(tokens) * lin_gain[...]).astype(BF16)
        weight_copies[0].wait()

        def act(n):
            lin = jnp.dot(normed, wv_qkv[n], preferred_element_type=F32)
            return (lin * jax.nn.sigmoid(lin)).astype(BF16).astype(F32)

        query, key, value = act(0), act(1), act(2)
        weight_copies[1].wait()
        gate = jax.nn.sigmoid(jnp.dot(normed, wv_gate[...], preferred_element_type=F32))
        query_t = jnp.transpose(query)
        key_t = jnp.transpose(key)
        total_of(relay_in, (rs_sem.at[0], rs_sem.at[1])).wait()
        for side in range(2):
            block = nexts[side][0]
            for b in range(half):
                acc[block, side * half + b] = acc[block, side * half + b] + relay_in[side, b]
            rs_copy(2, acc.at[block, parts[side]], rs_in.at[side, parts[side]], side).start()
        start_round(2)
        o_s[...] = jnp.zeros_like(o_s)

        def column(cols, p, b):
            lo = cols[2 * p * head_dim:(2 * p + 1) * head_dim, b:b + 1]
            hi = cols[(2 * p + 1) * head_dim:(2 * p + 2) * head_dim, b:b + 1]
            return jnp.where(low_half, lo, hi)

        total_of(rs_in, (rs_sem.at[2], rs_sem.at[3])).wait()

        for p in range(pairs):
            lam = jnp.exp(-pair_slope(p))
            cols = slice(p * LANES, (p + 1) * LANES)
            for b in range(rows):
                moved = acc[chip, b, p] + rs_in[0, b, p] + rs_in[1, b, p]
                state = lam * moved + column(key_t, p, b) * value[b:b + 1, cols]
                o_s[b:b + 1, cols] = jnp.sum(column(query_t, p, b) * state, axis=0, keepdims=True)
                st_out[b, 2 * p] = state[:, :head_dim]
                st_out[b, 2 * p + 1] = state[:, head_dim:]

        def tp_sum(buf, vals, sems):
            buf[me_tp] = vals
            copies = []
            for dt in (2, 1, 3)[-(tp_size - 1):]:
                copies.append(remote(buf.at[me_tp], buf.at[me_tp], sems.at[0], sems.at[1], {"tp": lax.rem(me_tp + dt, tp_size)}))
            for copy in copies:
                copy.start()
            total_of(buf.at[pl.ds(0, len(copies))], (sems.at[0], sems.at[1])).wait()
            total = buf[0]
            for n in range(1, tp_size):
                total = total + buf[n]
            return total

        wait_for_tp()
        lin_attn = o_s[...]
        squares = jnp.broadcast_to(jnp.sum(lin_attn * lin_attn, axis=-1, keepdims=True), (8, LANES))
        square_sum = tp_sum(sq_x, squares, sq_sem)[:, :1]
        mixed = (lin_attn * lax.rsqrt(square_sum / hidden_width + NORM_EPS) * out_gain[...] * gate).astype(BF16)
        weight_copies[2].wait()
        lin_out = tp_sum(y_x, jnp.dot(mixed, wv_lo[...], preferred_element_type=F32), y_sem)
        hidden = (normed.astype(F32) + lin_out).astype(BF16).astype(F32)
        normed_two = (rms(hidden) * attn_gain[...]).astype(BF16)

        weight_copies[3].wait()
        proj = lax.dot_general(normed_two, wv_in[...], NT, preferred_element_type=F32).astype(BF16).astype(F32)
        cols_in = proj.shape[1]
        quarter = head_dim // 4
        rotated = proj * rope[0:1, :] + pltpu.roll(proj, quarter, 1) * rope[1:2, :] + pltpu.roll(proj, cols_in - quarter, 1) * rope[2:3, :]
        rotated = rotated.astype(BF16).astype(F32)

        def segment_at(kv, segment):
            start = (kv * segments + segment) * head_dim
            block = rotated[:, start // LANES * LANES:start // LANES * LANES + LANES]
            if start % LANES != kv * head_dim:
                block = pltpu.roll(block, head_dim, 1)
            return jnp.where(low_half if kv == 0 else ~low_half, block, 0.0)

        def packed_at(segment):
            return (segment_at(0, segment) + segment_at(1, segment))[:rows]

        key_rows, value_rows = packed_at(group), packed_at(group + 1)
        for i in range(group):
            q_s[i * rows:(i + 1) * rows, :] = packed_at(i)
            kn_s[i * rows:(i + 1) * rows, :] = key_rows
            vn_s[i * rows:(i + 1) * rows, :] = value_rows

        def spread(vals):
            return jnp.concatenate([jnp.where(low_half, vals, 0.0), jnp.where(low_half, 0.0, vals)], axis=0)

        q_x[me] = q_s[...].astype(BF16)
        for dc in (2, 1, 3):
            remote(q_x.at[me], q_x.at[me], q_sem.at[0], q_sem.at[1], {"sp": peer_index(dc, 0)}).start()
        remote(q_x.at[me], q_x.at[me], q_sem.at[2], q_sem.at[3], partner).start()
        start_round(3)
        start_round(4)

        def shard_copies(j, slot):
            return [pltpu.make_async_copy(cache.at[pl.ds(j * rows, rows)], buf.at[slot], kb_sem.at[n, slot])
                    for n, (cache, buf) in enumerate(((k_in, k_buf), (v_in, v_buf)))]

        for copy in shard_copies(0, 0):
            copy.start()

        rotated_t = jnp.transpose(rotated)
        lane16 = lax.broadcasted_iota(jnp.int32, (1, CACHE_EXTRA), 1)
        prompt_len = sp_size * shard_len
        for land, segment in ((k_land, group), (v_land, group + 1)):
            for kv in range(kv_dev):
                start = (kv * segments + segment) * head_dim
                for b in range(rows):
                    tail = jnp.where(lane16 == 0, rotated_t[start:start + head_dim, b:b + 1], 0.0)
                    land[b, kv, :, prompt_len:] = tail.astype(BF16)

        row_id = lax.broadcasted_iota(jnp.int32, (qrows, 1), 0)
        row_seq = lax.rem(row_id, rows)
        split = group * rows
        scale = head_dim ** -0.5

        total_of(q_x.at[pl.ds(0, chips - 1)], (q_sem.at[0], q_sem.at[1])).wait()
        for dc in (2, 1, 3):
            src = peer_index(dc, 0)
            remote(q_x.at[src], q_x.at[src], q_sem.at[2], q_sem.at[3], partner).start()
        total_of(q_x.at[pl.ds(0, chips)], (q_sem.at[2], q_sem.at[3])).wait()

        def write_partial(ref, out, peak, total):
            ref[:split] = out
            stats = jnp.transpose(jnp.where(low_half, peak, total))
            stats = jnp.concatenate([stats[:4], stats[head_dim:head_dim + 4]], axis=0)
            ref[split:] = jnp.concatenate([stats, jnp.zeros((8, LANES - qrows), F32)], axis=1)

        def read_partial(ref):
            stats = jnp.transpose(ref[split:])
            return ref[:split], stats[:qrows, 0:1], stats[:qrows, 4:5]

        def both_heads(column_vals):
            return jnp.where(low_half, column_vals[:split], column_vals[split:])

        @pl.loop(0, sp_size)
        def _(j):
            slot = lax.rem(j, 2)

            @pl.when(j + 1 < sp_size)
            def _():
                for copy in shard_copies(j + 1, lax.rem(j + 1, 2)):
                    copy.start()

            for copy in shard_copies(j, slot):
                copy.wait()
            queries = spread(q_x[j].astype(F32)).astype(BF16)
            scores = jnp.zeros((qrows, shard_len), F32)
            for b in range(rows):
                keys = k_buf[slot, b].reshape(kv_dev * head_dim, shard_len)
                scores = jnp.where(row_seq == b, jnp.dot(queries, keys, preferred_element_type=F32), scores)
            scores = scores * scale
            peak = jnp.max(scores, axis=-1, keepdims=True)
            probs = jnp.exp(scores - peak)
            total = jnp.sum(probs, axis=-1, keepdims=True)
            probs = probs.astype(BF16)
            out = jnp.zeros((qrows, LANES), F32)
            for b in range(rows):
                vals = v_buf[slot, b].reshape(kv_dev * head_dim, shard_len)
                out = jnp.where(row_seq == b, lax.dot_general(probs, vals, NT, preferred_element_type=F32), out)
            write_partial(pr_out.at[lax.rem(j, 2), j // 2], both_heads(out), peak, total)

        pr_swap = remote(pr_out.at[1 - core], pr_pair, pr_sem.at[0], pr_sem.at[1], partner)
        pr_swap.start()
        pr_swap.wait()

        @pl.loop(0, chips)
        def _(block):
            out_a, peak_a, total_a = read_partial(pr_out.at[core, block])
            out_b, peak_b, total_b = read_partial(pr_pair.at[block])
            peak = jnp.maximum(peak_a, peak_b)
            scale_a, scale_b = jnp.exp(peak_a - peak), jnp.exp(peak_b - peak)
            write_partial(pr_mine.at[block], out_a * both_heads(scale_a) + out_b * both_heads(scale_b), peak, total_a * scale_a + total_b * scale_b)

        for dc in (2, 1, 3):
            dst_chip = lax.rem(chip + dc, chips)
            remote(pr_mine.at[dst_chip], pr_in.at[chip], pr_sem.at[2], pr_sem.at[3], {"sp": dst_chip * 2 + core}).start()
        for round_idx in range(5, 2 * rows):
            start_round(round_idx)
        pr_in[chip] = pr_mine[chip]

        new_score = jnp.sum(spread(q_s[...] * kn_s[...]), axis=-1, keepdims=True) * scale

        total_of(pr_in.at[pl.ds(0, chips - 1)], (pr_sem.at[2], pr_sem.at[3])).wait()
        partials = [read_partial(pr_in.at[n]) for n in range(chips)]
        top = new_score
        for _, peak, _ in partials:
            top = jnp.maximum(top, peak)
        new_prob = jnp.exp(new_score - top)
        prob_sum = new_prob
        head = new_prob.astype(BF16).astype(F32) * spread(vn_s[...])
        for out, peak, total in partials:
            weight = jnp.exp(peak - top)
            prob_sum = prob_sum + weight * total
            head = head + weight * spread(out)
        head = (head / prob_sum).astype(BF16).astype(F32)

        ho_s[...] = jnp.zeros_like(ho_s)
        for n in range(0, kv_dev * group, 2):
            block = None
            for m in (n, n + 1):
                kv = m // group
                piece = head[m * rows:(m + 1) * rows]
                if kv != m % 2:
                    piece = pltpu.roll(piece, head_dim, 1)
                block = piece if block is None else block + piece
            ho_s[0:rows, n // 2 * LANES:(n // 2 + 1) * LANES] = block
        weight_copies[4].wait()
        attn_out = tp_sum(a_x, jnp.dot(ho_s[...].astype(BF16), wv_ao[...], preferred_element_type=F32), a_sem)
        hid_out[...] = (normed_two.astype(F32) + attn_out).astype(BF16)[:rows]

        for copy in own_copies:
            copy.wait()
        for n, cache in enumerate((k_in, v_in)):
            total_of(cache.at[pl.ds(0, len(peers) * rows)], (kv_send.at[n], kv_recv.at[n])).wait()

    dma = pltpu.SemaphoreType.DMA
    pl.run_scoped(decode_step, dma((6,)), dma((5,)), dma((2,)), dma((2,)), dma((2, 2)))


def put_kernel(*refs):
    count = (len(refs) - 1) // 2
    sems = refs[-1]
    copies = []
    for n in (2, 3, 1, 0):
        pieces = refs[n].shape[0] if n > 0 else 1
        for i in range(pieces):
            src, dst = (refs[n].at[i], refs[count + n].at[i]) if pieces > 1 else (refs[n], refs[count + n])
            copies.append(pltpu.make_async_copy(src, dst, sems.at[len(copies)]))
    for copy in copies:
        copy.start()
    for copy in copies:
        copy.wait()


def solution(mesh):
    sp_size = mesh.shape['sp']
    tp_size = mesh.shape['tp']
    chips = sp_size // 2

    def device_step(tokens, states, k_cache, v_cache, slopes, lin_gain, w_lin_qkv, w_lin_gate, out_gain, w_lin_out, attn_gain, w_attn_in, w_attn_out):
        rows, model = tokens.shape
        kv_dev, shard_len, head_dim = k_cache.shape[1:]
        heads = slopes.shape[0]
        segments = w_attn_in.shape[2]
        group = segments - 2
        width = heads * head_dim
        pairs = heads // 2
        cols_in = kv_dev * segments * head_dim
        qrows = kv_dev * group * rows
        prompt_len = sp_size * shard_len
        full_len = prompt_len + CACHE_EXTRA
        dims = (chips, tp_size, rows, heads, head_dim, kv_dev, group, shard_len)
        rope = jnp.asarray(rope_tables(kv_dev, segments, group, head_dim, prompt_len))

        vmem = pl.BlockSpec(memory_space=pltpu.VMEM)
        anym = pl.BlockSpec(memory_space=pl.ANY)
        dma = pltpu.SemaphoreType.DMA
        land_shape = (rows, kv_dev, head_dim, full_len)
        out_types = [((rows, model), BF16), ((rows, heads, head_dim, head_dim), F32), (land_shape, BF16), (land_shape, BF16)]
        scratch = [
            pltpu.SMEM((heads,), F32),
            pltpu.VMEM((rows, model), BF16),
            pltpu.VMEM((1, model), F32),
            pltpu.VMEM((1, width), F32),
            pltpu.VMEM((1, model), F32),
            pltpu.VMEM((8, cols_in), F32),
            pltpu.VMEM((3, model, width), BF16),
            pltpu.VMEM((model, width), BF16),
            pltpu.VMEM((width, model), BF16),
            pltpu.VMEM((cols_in, model), BF16),
            pltpu.VMEM((width, model), BF16),
            pltpu.VMEM((2, rows, heads, head_dim, head_dim), F32),
            pltpu.VMEM((chips, rows, pairs, head_dim, LANES), F32),
            pltpu.VMEM((chips, rows, pairs, head_dim, LANES), F32),
            pltpu.VMEM((chips, rows, pairs, head_dim, LANES), F32),
            pltpu.VMEM((2, rows // 2, pairs, head_dim, LANES), F32),
            pltpu.VMEM((2, rows, pairs, head_dim, LANES), F32),
            pltpu.VMEM((tp_size, 8, LANES), F32),
            pltpu.VMEM((tp_size, 8, model), F32),
            pltpu.VMEM((tp_size, 8, model), F32),
            pltpu.VMEM((sp_size, group * rows, LANES), BF16),
            pltpu.VMEM((2, chips, group * rows + 8, LANES), F32),
            pltpu.VMEM((chips, group * rows + 8, LANES), F32),
            pltpu.VMEM((chips, group * rows + 8, LANES), F32),
            pltpu.VMEM((chips, group * rows + 8, LANES), F32),
            pltpu.VMEM((2, rows, kv_dev, head_dim, shard_len), BF16),
            pltpu.VMEM((2, rows, kv_dev, head_dim, shard_len), BF16),
            pltpu.VMEM((8, width), F32),
            pltpu.VMEM((group * rows, LANES), F32),
            pltpu.VMEM((group * rows, LANES), F32),
            pltpu.VMEM((group * rows, LANES), F32),
            pltpu.VMEM((8, width), F32),
            pltpu.SemaphoreType.REGULAR,
            dma((2,)),
            dma((4,)),
            dma((2,)),
            dma((2,)),
            dma((2,)),
            dma((4,)),
            dma((4,)),
            dma((2,)),
            dma((2,)),
        ]
        landed = pl.pallas_call(
            functools.partial(step_kernel, dims),
            out_shape=[pltpu.VMEM(shape, dtype) for shape, dtype in out_types],
            in_specs=[anym, anym, anym, anym, anym, anym] + [anym] * 8,
            out_specs=[vmem] * 4,
            scratch_shapes=scratch,
            compiler_params=pltpu.CompilerParams(collective_id=0, has_side_effects=True, vmem_limit_bytes=40 * 2 ** 20),
        )(
            tokens, slopes, lin_gain.reshape(1, -1), out_gain.reshape(1, -1), attn_gain.reshape(1, -1), rope,
            states, jnp.transpose(k_cache, (0, 1, 3, 2)), jnp.transpose(v_cache, (0, 1, 3, 2)),
            jnp.transpose(w_lin_qkv, (1, 0, 2)), w_lin_gate, w_lin_out,
            jnp.transpose(w_attn_in, (1, 2, 3, 0)).reshape(cols_in, model), w_attn_out,
        )
        hidden_out, state_new, k_out, v_out = pl.pallas_call(
            put_kernel,
            out_shape=[jax.ShapeDtypeStruct(shape, dtype) for shape, dtype in out_types],
            in_specs=[vmem] * 4,
            out_specs=[anym] * 4,
            scratch_shapes=[dma((3 * rows + 1,))],
            compiler_params=pltpu.CompilerParams(vmem_limit_bytes=2 * 2 ** 20),
        )(*landed)
        return hidden_out, state_new, jnp.transpose(k_out, (0, 1, 3, 2)), jnp.transpose(v_out, (0, 1, 3, 2))

    batch_spec = P(('dp', 'sp'), None)
    head_spec = P(('dp', 'sp'), 'tp', None, None)
    cache_spec = P('dp', 'tp', 'sp', None)
    in_specs = (batch_spec, P('sp', 'dp', 'tp', None, None), cache_spec, cache_spec, P('tp'), P(None), P(None, None, 'tp'), P(None, 'tp'), P('tp'), P('tp', None), P(None), P(None, 'tp', None, None), P('tp', None))
    out_specs = (batch_spec, head_spec, head_spec, head_spec)
    return jax.shard_map(device_step, mesh=mesh, in_specs=in_specs, out_specs=out_specs, check_vma=False)
```

time: 373 us -> 211 us (0.57)
  the two profiles are of different devices: /device:TPU:96 before, /device:TPU:97 now
where the time goes in v4:
time: 211 us
  Pallas kernels  210 us (100%)
    pallas_call x1, Pallas kernels, device_step(): pl.pallas_call(functools.partial(step_kernel, dims), out_shape=[pltpu.VME...  204 us
    pallas_call x1, Pallas kernels, device_step(): pl.pallas_call(put_kernel, out_shape=[jax.ShapeDtypeStruct(shape, dtype)...  6.3 us

profile of v4, /device:TPU:97, one launch (start us, length us, event | category | flops | bytes accessed | tf_op | source)
XLA Modules:
  0.0 210.6 jit_solution(10997676393151503269)
XLA Ops:
  0.6 203.6 %shard_map.165 = (bf16[4,2048]{1,0:T(4,128)(2,1)S(1)}, f32[4,8,64,64]{3,2,1,0:T(8,128)S(1)}, bf16[4,2,64,8208]{3,2,1,0:T(8,128)(2,1)S(1)}, bf16[4,2,64,8208]{3,2,1,0:T(8,128)(2,1)S(1)}) custom-call(bf16[4,2048]{1,0:T(4,128)(2,1)} %tok_in.1, f32[8]{0:T(128)} %slopes_in.1, f32[1,2048]{1,0:T(1,128)} %bitcast.15, f32[1,512]{1,0:T(1,128)} %bitcast.17, ...), custom_call_target="tpu_custom_call" | custom-call | tf_op jit(solution)/shard_map/pallas_call | solution.py:505
  204.3 6.3 %shard_map.166 = (bf16[4,2048]{1,0:T(4,128)(2,1)}, f32[4,8,64,64]{3,2,1,0:T(8,128)}, bf16[4,2,64,8208]{3,2,1,0:T(8,128)(2,1)}, bf16[4,2,64,8208]{3,2,1,0:T(8,128)(2,1)}) custom-call(bf16[4,2048]{1,0:T(4,128)(2,1)S(1)} %get-tuple-element.12.refs_0_, f32[4,8,64,64]{3,2,1,0:T(8,128)S(1)} %get-tuple-element.13.refs_1_, ...), custom_call_target="tpu_custom_call" | custom-call | tf_op jit(solution)/shard_map/pallas_call | solution.py:518

commit v5 on v4

--- a/solution.py
+++ b/solution.py
@@ -36,10 +36,10 @@
 
 
 def step_kernel(dims, tok_in, slopes_in, lin_gain_in, out_gain_in, attn_gain_in, rope_in, states, k_in, v_in, w_qkv, w_gate, w_lo, w_in, w_ao,
-                hid_out, st_out, k_land, v_land,
+                hid_out, st_out, k_land, v_land, k_swap, v_swap,
                 slopes, tok, lin_gain, out_gain, attn_gain, rope, wv_qkv, wv_gate, wv_lo, wv_in, wv_ao, st_buf, p_out, p_in, acc, relay_in, rs_in, sq_x, y_x, a_x, q_x, pr_out, pr_pair, pr_mine, pr_in,
                 k_buf, v_buf, o_s, q_s, kn_s, vn_s, ho_s,
-                go_sem, pair_sem, rs_sem, sq_sem, y_sem, a_sem, q_sem, pr_sem, kv_send, kv_recv):
+                go_sem, pair_sem, rs_sem, sq_sem, y_sem, a_sem, q_sem, pr_sem, kv_send, kv_recv, swap_sem):
     chips, tp_size, rows, heads, head_dim, kv_dev, group, shard_len = dims
     sp_size = 2 * chips
     pairs = heads // 2
@@ -53,24 +53,25 @@
     me_tp = lax.axis_index("tp")
     chip = me // 2
     core = lax.rem(me, 2)
-    peers = [(dc, cr) for dc, cr in ((2, 0), (1, 0), (3, 0), (2, 1), (1, 1), (3, 1), (0, 1))]
-
-    def peer_index(dc, cr):
-        return lax.rem(chip + dc, chips) * 2 + (core if cr == 0 else 1 - core)
+    steps = (2, 1, 3)
+
+    def same_core(dc):
+        return lax.rem(chip + dc, chips) * 2 + core
 
     barrier = pltpu.get_barrier_semaphore()
-    for dc, cr in peers:
-        pl.semaphore_signal(barrier, inc=1, device_id={"sp": peer_index(dc, cr)}, device_id_type=MESH)
+    for dc in steps:
+        pl.semaphore_signal(barrier, inc=1, device_id={"sp": same_core(dc)}, device_id_type=MESH)
+    pl.semaphore_signal(barrier, inc=1, device_id={"sp": chip * 2 + (1 - core)}, device_id_type=MESH)
 
     @pl.when(me_tp == 0)
     def _():
-        pl.semaphore_wait(barrier, len(peers))
+        pl.semaphore_wait(barrier, chips)
         for other in range(1, tp_size):
             pl.semaphore_signal(barrier, inc=1, device_id={"tp": other}, device_id_type=MESH)
 
     @pl.when(me_tp != 0)
     def _():
-        pl.semaphore_wait(barrier, len(peers) + 1)
+        pl.semaphore_wait(barrier, chips + 1)
         pl.semaphore_signal(barrier, inc=1, device_id={"tp": 0}, device_id_type=MESH)
 
     def wait_for_tp():
@@ -90,23 +91,25 @@
     partner = {"sp": chip * 2 + (1 - core)}
     my_cols = pl.ds(pl.multiple_of(me * shard_len, LANES), shard_len)
 
-    def kv_copies(round_idx):
-        cache, land = ((k_in, k_land), (v_in, v_land))[round_idx % 2]
-        row = round_idx // 2
-        copies = []
-        for n, (dc, cr) in enumerate(peers):
-            dst = peer_index(dc, cr)
-            copies.append(remote(cache.at[dst * rows + row], land.at[row, :, :, my_cols], kv_send.at[round_idx % 2], kv_recv.at[round_idx % 2], {"sp": dst}))
-        return copies
-
-    def start_round(round_idx):
-        for copy in kv_copies(round_idx):
-            copy.start()
+    partner_cols = pl.ds(pl.multiple_of((chip * 2 + (1 - core)) * shard_len, LANES), shard_len)
+
+    def start_round(round_idx, own):
+        which, row = round_idx % 2, round_idx // 2
+        cache, swap, land = ((k_in, k_swap, k_land), (v_in, v_swap, v_land))[which]
+        for dc in steps:
+            dst = same_core(dc)
+            src, cols = (cache.at[dst * rows + row], my_cols) if own else (swap.at[lax.rem(chip + dc, chips) * rows + row], partner_cols)
+            remote(src, land.at[row, :, :, cols], kv_send.at[which], kv_recv.at[which], {"sp": dst}).start()
 
     def total_of(ref, sems):
         return remote(ref, ref, sems[0], sems[1], partner)
 
-    start_round(0)
+    start_round(0, True)
+    for cache, swap, n in ((k_in, k_swap, 0), (v_in, v_swap, 1)):
+        for block in range(chips):
+            src = cache.at[pl.ds((block * 2 + (1 - core)) * rows, rows)]
+            remote(src, swap.at[pl.ds(block * rows, rows)], swap_sem.at[2 * n], swap_sem.at[2 * n + 1], partner).start()
+    start_round(1, True)
 
     def decode_step(in_sem, w_sem, st_sem, own_sem, kb_sem):
         def state_copy(step, slot):
@@ -165,6 +168,13 @@
                       for n, (cache, land) in enumerate(((k_in, k_land), (v_in, v_land)))]
         for copy in own_copies:
             copy.start()
+        for n, swap in enumerate((k_swap, v_swap)):
+            total_of(swap, (swap_sem.at[2 * n], swap_sem.at[2 * n + 1])).wait()
+        partner_copies = [pltpu.make_async_copy(swap.at[pl.ds(chip * rows, rows)], land.at[:, :, :, partner_cols], own_sem.at[2 + n])
+                          for n, (swap, land) in enumerate(((k_swap, k_land), (v_swap, v_land)))]
+        for copy in partner_copies:
+            copy.start()
+        start_round(0, False)
 
         pair_copy.wait()
 
@@ -185,7 +195,7 @@
         rs_copies = [rs_copy(2, acc.at[nexts[side][0], parts[1 - side]], rs_in.at[side, parts[1 - side]], side) for side in range(2)]
         for copy in relay_copies + rs_copies:
             copy.start()
-        start_round(1)
+        start_round(1, False)
 
         def rms(vals):
             return vals * lax.rsqrt(jnp.mean(vals * vals, axis=-1, keepdims=True) + NORM_EPS)
@@ -216,7 +226,8 @@
             for b in range(half):
                 acc[block, side * half + b] = acc[block, side * half + b] + relay_in[side, b]
             rs_copy(2, acc.at[block, parts[side]], rs_in.at[side, parts[side]], side).start()
-        start_round(2)
+        start_round(2, True)
+        start_round(2, False)
         o_s[...] = jnp.zeros_like(o_s)
 
         def column(cols, p, b):
@@ -286,11 +297,13 @@
             return jnp.concatenate([jnp.where(low_half, vals, 0.0), jnp.where(low_half, 0.0, vals)], axis=0)
 
         q_x[me] = q_s[...].astype(BF16)
-        for dc in (2, 1, 3):
-            remote(q_x.at[me], q_x.at[me], q_sem.at[0], q_sem.at[1], {"sp": peer_index(dc, 0)}).start()
+        for dc in steps:
+            remote(q_x.at[me], q_x.at[me], q_sem.at[0], q_sem.at[1], {"sp": same_core(dc)}).start()
         remote(q_x.at[me], q_x.at[me], q_sem.at[2], q_sem.at[3], partner).start()
-        start_round(3)
-        start_round(4)
+        for own in (True, False):
+            start_round(3, own)
+        for own in (True, False):
+            start_round(4, own)
 
         def shard_copies(j, slot):
             return [pltpu.make_async_copy(cache.at[pl.ds(j * rows, rows)], buf.at[slot], kb_sem.at[n, slot])
@@ -316,7 +329,7 @@
 
         total_of(q_x.at[pl.ds(0, chips - 1)], (q_sem.at[0], q_sem.at[1])).wait()
         for dc in (2, 1, 3):
-            src = peer_index(dc, 0)
+            src = same_core(dc)
             remote(q_x.at[src], q_x.at[src], q_sem.at[2], q_sem.at[3], partner).start()
         total_of(q_x.at[pl.ds(0, chips)], (q_sem.at[2], q_sem.at[3])).wait()
 
@@ -375,8 +388,14 @@
         for dc in (2, 1, 3):
             dst_chip = lax.rem(chip + dc, chips)
             remote(pr_mine.at[dst_chip], pr_in.at[chip], pr_sem.at[2], pr_sem.at[3], {"sp": dst_chip * 2 + core}).start()
-        for round_idx in range(5, 2 * rows):
-            start_round(round_idx)
+        for own in (True, False):
+            start_round(5, own)
+
+        @pl.when(core == 1)
+        def _():
+            for own in (True, False):
+                start_round(6, own)
+
         pr_in[chip] = pr_mine[chip]
 
         new_score = jnp.sum(spread(q_s[...] * kn_s[...]), axis=-1, keepdims=True) * scale
@@ -411,11 +430,72 @@
 
         for copy in own_copies:
             copy.wait()
-        for n, cache in enumerate((k_in, v_in)):
-            total_of(cache.at[pl.ds(0, len(peers) * rows)], (kv_send.at[n], kv_recv.at[n])).wait()
+        for copy in partner_copies:
+            copy.wait()
+        blocks = 2 * (chips - 1)
+        total_of(v_in.at[pl.ds(0, blocks * (rows - 1))], (kv_send.at[1], kv_recv.at[1])).wait()
+
+        @pl.when(core == 0)
+        def _():
+            total_of(k_in.at[pl.ds(0, blocks * (rows - 1))], (kv_send.at[0], kv_recv.at[0])).wait()
+
+        @pl.when(core == 1)
+        def _():
+            total_of(k_in.at[pl.ds(0, blocks * rows)], (kv_send.at[0], kv_recv.at[0])).wait()
 
     dma = pltpu.SemaphoreType.DMA
-    pl.run_scoped(decode_step, dma((6,)), dma((5,)), dma((2,)), dma((2,)), dma((2, 2)))
+    pl.run_scoped(decode_step, dma((6,)), dma((5,)), dma((2,)), dma((4,)), dma((2, 2)))
+
+
+def last_kernel(dims, k_in, v_in, k_swap, v_swap, _, k_last, v_last, kv_send, kv_recv, own_sem):
+    chips, _, rows, _, _, _, _, shard_len = dims
+    me = lax.axis_index("sp")
+    chip = me // 2
+    core = lax.rem(me, 2)
+    row = rows - 1
+
+    def same_core(dc):
+        return lax.rem(chip + dc, chips) * 2 + core
+
+    barrier = pltpu.get_barrier_semaphore()
+    for dc in (2, 1, 3):
+        pl.semaphore_signal(barrier, inc=1, device_id={"sp": same_core(dc)}, device_id_type=MESH)
+    pl.semaphore_wait(barrier, chips - 1)
+    my_cols = pl.ds(pl.multiple_of(me * shard_len, LANES), shard_len)
+    partner_cols = pl.ds(pl.multiple_of((chip * 2 + (1 - core)) * shard_len, LANES), shard_len)
+
+    def own_copies(n, cache, swap, last):
+        return [pltpu.make_async_copy(cache.at[me * rows + row], last.at[:, :, my_cols], own_sem.at[2 * n]),
+                pltpu.make_async_copy(swap.at[chip * rows + row], last.at[:, :, partner_cols], own_sem.at[2 * n + 1])]
+
+    def start(n, cache, swap, last):
+        for own in (True, False):
+            for dc in (2, 1, 3):
+                dst = same_core(dc)
+                src, cols = (cache.at[dst * rows + row], my_cols) if own else (swap.at[lax.rem(chip + dc, chips) * rows + row], partner_cols)
+                pltpu.make_async_remote_copy(src_ref=src, dst_ref=last.at[:, :, cols], send_sem=kv_send.at[n], recv_sem=kv_recv.at[n], device_id={"sp": dst}, device_id_type=MESH).start()
+        for copy in own_copies(n, cache, swap, last):
+            copy.start()
+
+    def finish(n, cache, swap, last):
+        for copy in own_copies(n, cache, swap, last):
+            copy.wait()
+        ref = cache.at[pl.ds(0, 2 * (chips - 1))]
+        pltpu.make_async_remote_copy(src_ref=ref, dst_ref=ref, send_sem=kv_send.at[n], recv_sem=kv_recv.at[n], device_id={"sp": same_core(1)}, device_id_type=MESH).wait()
+
+    k_args, v_args = (0, k_in, k_swap, k_last), (1, v_in, v_swap, v_last)
+
+    @pl.when(core == 0)
+    def _():
+        start(*k_args)
+
+    start(*v_args)
+
+    @pl.when(core == 0)
+    def _():
+        finish(*k_args)
+
+    finish(*v_args)
 
 
 def put_kernel(*refs):
@@ -431,6 +511,22 @@
         copy.start()
     for copy in copies:
         copy.wait()
+
+
+def put_last_kernel(k_first, v_first, k_last, v_last, k_dst, v_dst, sems):
+    row = k_dst.shape[0] - 1
+    cols = pl.ds(0, k_last.shape[-1])
+    k_copy = pltpu.make_async_copy(k_last, k_dst.at[row, :, :, cols], sems.at[0])
+    v_copy = pltpu.make_async_copy(v_last, v_dst.at[row, :, :, cols], sems.at[1])
+    has_k = lax.rem(lax.axis_index("sp"), 2) == 0
+    v_copy.start()
+
+    @pl.when(has_k)
+    def _():
+        k_copy.start()
+        k_copy.wait()
+
+    v_copy.wait()
 
 
 def solution(mesh):
@@ -455,7 +551,12 @@
 
         vmem = pl.BlockSpec(memory_space=pltpu.VMEM)
         anym = pl.BlockSpec(memory_space=pl.ANY)
+        hbm = pl.BlockSpec(memory_space=pltpu.HBM)
         dma = pltpu.SemaphoreType.DMA
+
+        def in_hbm(*arrays):
+            return [pltpu.with_memory_space_constraint(array, pltpu.HBM) for array in arrays]
+
         land_shape = (rows, kv_dev, head_dim, full_len)
         out_types = [((rows, model), BF16), ((rows, heads, head_dim, head_dim), F32), (land_shape, BF16), (land_shape, BF16)]
         scratch = [
@@ -501,17 +602,20 @@
             dma((4,)),
             dma((2,)),
             dma((2,)),
+            dma((4,)),
         ]
-        landed = pl.pallas_call(
+        k_cols, v_cols = jnp.transpose(k_cache, (0, 1, 3, 2)), jnp.transpose(v_cache, (0, 1, 3, 2))
+        swap_type = jax.ShapeDtypeStruct((chips * rows, kv_dev, head_dim, shard_len), BF16)
+        *landed, k_swap, v_swap = pl.pallas_call(
             functools.partial(step_kernel, dims),
-            out_shape=[pltpu.VMEM(shape, dtype) for shape, dtype in out_types],
+            out_shape=[pltpu.VMEM(shape, dtype) for shape, dtype in out_types] + [swap_type] * 2,
             in_specs=[anym, anym, anym, anym, anym, anym] + [anym] * 8,
-            out_specs=[vmem] * 4,
+            out_specs=[vmem] * 4 + [anym] * 2,
             scratch_shapes=scratch,
             compiler_params=pltpu.CompilerParams(collective_id=0, has_side_effects=True, vmem_limit_bytes=40 * 2 ** 20),
         )(
             tokens, slopes, lin_gain.reshape(1, -1), out_gain.reshape(1, -1), attn_gain.reshape(1, -1), rope,
-            states, jnp.transpose(k_cache, (0, 1, 3, 2)), jnp.transpose(v_cache, (0, 1, 3, 2)),
+            states, k_cols, v_cols,
             jnp.transpose(w_lin_qkv, (1, 0, 2)), w_lin_gate, w_lin_out,
             jnp.transpose(w_attn_in, (1, 2, 3, 0)).reshape(cols_in, model), w_attn_out,
         )
@@ -523,6 +627,24 @@
             scratch_shapes=[dma((3 * rows + 1,))],
             compiler_params=pltpu.CompilerParams(vmem_limit_bytes=2 * 2 ** 20),
         )(*landed)
+        last_shape = (kv_dev, head_dim, prompt_len)
+        last_rows = pl.pallas_call(
+            functools.partial(last_kernel, dims),
+            out_shape=[pltpu.VMEM(last_shape, BF16)] * 2,
+            in_specs=[hbm] * 5,
+            out_specs=[vmem] * 2,
+            scratch_shapes=[dma((2,)), dma((2,)), dma((4,))],
+            compiler_params=pltpu.CompilerParams(collective_id=1, has_side_effects=True, vmem_limit_bytes=2 * 2 ** 20),
+        )(*in_hbm(k_cols, v_cols, k_swap, v_swap, hidden_out))
+        k_out, v_out = pl.pallas_call(
+            put_last_kernel,
+            out_shape=[jax.ShapeDtypeStruct(shape, dtype) for shape, dtype in out_types[2:]],
+            in_specs=[hbm] * 2 + [vmem] * 2,
+            out_specs=[hbm] * 2,
+            scratch_shapes=[dma((2,))],
+            input_output_aliases={0: 0, 1: 1},
+            compiler_params=pltpu.CompilerParams(vmem_limit_bytes=2 * 2 ** 20),
+        )(*in_hbm(k_out, v_out), *last_rows)
         return hidden_out, state_new, jnp.transpose(k_out, (0, 1, 3, 2)), jnp.transpose(v_out, (0, 1, 3, 2))
 
     batch_spec = P(('dp', 'sp'), None)

time: 211 us -> 208 us (0.986)
  Pallas kernels: 210 us -> 205 us
    pallas_call x1, Pallas kernels: 204 us -> 169 us  [device_step(): pl.pallas_call(functools.partial(step_kernel, dims), out_shape=[pltpu.VME...]
    pallas_call x0 -> x2, Pallas kernels: none -> 29.7 us  [the longest x1 28.4 us: device_step(): pl.pallas_call(functools.partial(last_kernel, dims), out_shape=[pltpu.VME...]
where the time goes in v5:
time: 208 us; the launch traced here: 206 us
  Pallas kernels  205 us (99%)
    pallas_call x1, Pallas kernels, device_step(): pl.pallas_call(functools.partial(step_kernel, dims), out_shape=[pltpu.VME...  169 us
    pallas_call x1, Pallas kernels, device_step(): pl.pallas_call(functools.partial(last_kernel, dims), out_shape=[pltpu.VME...  28.4 us
    pallas_call x1, Pallas kernels, device_step(): pl.pallas_call(put_kernel, out_shape=[jax.ShapeDtypeStruct(shape, dtype)...  6.3 us

profile of v5, /device:TPU:97, one launch (start us, length us, event | category | flops | bytes accessed | tf_op | source)
XLA Modules:
  0.0 206.0 jit_solution(10806068666660571575)
XLA Ops:
  0.6 169.3 %shard_map.165 = (bf16[4,2048]{1,0:T(4,128)(2,1)S(1)}, f32[4,8,64,64]{3,2,1,0:T(8,128)S(1)}, bf16[4,2,64,8208]{3,2,1,0:T(8,128)(2,1)S(1)}, bf16[4,2,64,8208]{3,2...) custom-call(bf16[4,2048]{1,0:T(4,128)(2,1)} %tok_in.1, f32[8]{0:T(128)} %slopes_in.1, ...), custom_call_target="tpu_custom_call" | custom-call | tf_op jit(solution)/shard_map/pallas_call | solution.py:609
  170.0 6.3 %shard_map.166 = (bf16[4,2048]{1,0:T(4,128)(2,1)}, f32[4,8,64,64]{3,2,1,0:T(8,128)}, bf16[4,2,64,8208]{3,2,1,0:T(8,128)(2,1)}, bf16[4,2,64,8208]{3,2,1,0:T(8,128)(2,1)}) custom-call(bf16[4,2048]{1,0:T(4,128)(2,1)S(1)} %get-tuple-element.18.refs_0_, f32[4,8,64,64]{3,2,1,0:T(8,128)S(1)} %get-tuple-element.19.refs_1_, ...), custom_call_target="tpu_custom_call" | custom-call | tf_op jit(solution)/shard_map/pallas_call | solution.py:622
  176.3 28.4 %shard_map.167 = (bf16[2,64,8192]{2,1,0:T(8,128)(2,1)S(1)}, bf16[2,64,8192]{2,1,0:T(8,128)(2,1)S(1)}) custom-call(bf16[32,2,64,1024]{3,2,1,0:T(8,128)(2,1)} %bitcast.12, bf16[32,2,64,1024]{3,2,1,0:T(8,128)(2,1)} %bitcast.14, bf16[16,2,64,1024]{3,2,1,0:T(8,128)(2,1)} %get-tuple-element.26.k_swap, bf16[16,2,64,1024]{3,2,1,0:T(8,128)(2,1)} %get-tuple-element.27.v_swap, ...), custom_call_target="tpu_custom_call" | custom-call | tf_op jit(solution)/shard_map/pallas_call | solution.py:631
  204.7 1.3 shard_map.168

commit v6 on v5

--- a/solution.py
+++ b/solution.py
@@ -94,7 +94,7 @@
     partner_cols = pl.ds(pl.multiple_of((chip * 2 + (1 - core)) * shard_len, LANES), shard_len)
 
     def start_round(round_idx, own):
-        which, row = round_idx % 2, round_idx // 2
+        which, row = ((0, 0), (1, 0), (0, 1), (1, 1), (1, 2), (1, 3), (0, 2))[round_idx]
         cache, swap, land = ((k_in, k_swap, k_land), (v_in, v_swap, v_land))[which]
         for dc in steps:
             dst = same_core(dc)
@@ -433,26 +433,25 @@
         for copy in partner_copies:
             copy.wait()
         blocks = 2 * (chips - 1)
-        total_of(v_in.at[pl.ds(0, blocks * (rows - 1))], (kv_send.at[1], kv_recv.at[1])).wait()
+        total_of(v_in.at[pl.ds(0, blocks * rows)], (kv_send.at[1], kv_recv.at[1])).wait()
 
         @pl.when(core == 0)
         def _():
-            total_of(k_in.at[pl.ds(0, blocks * (rows - 1))], (kv_send.at[0], kv_recv.at[0])).wait()
+            total_of(k_in.at[pl.ds(0, blocks * (rows - 2))], (kv_send.at[0], kv_recv.at[0])).wait()
 
         @pl.when(core == 1)
         def _():
-            total_of(k_in.at[pl.ds(0, blocks * rows)], (kv_send.at[0], kv_recv.at[0])).wait()
+            total_of(k_in.at[pl.ds(0, blocks * (rows - 1))], (kv_send.at[0], kv_recv.at[0])).wait()
 
     dma = pltpu.SemaphoreType.DMA
     pl.run_scoped(decode_step, dma((6,)), dma((5,)), dma((2,)), dma((4,)), dma((2, 2)))
 
 
-def last_kernel(dims, k_in, v_in, k_swap, v_swap, _, k_last, v_last, kv_send, kv_recv, own_sem):
+def last_kernel(dims, k_in, k_swap, _, k_last, k_send, k_recv, own_sem):
     chips, _, rows, _, _, _, _, shard_len = dims
     me = lax.axis_index("sp")
     chip = me // 2
     core = lax.rem(me, 2)
-    row = rows - 1
 
     def same_core(dc):
         return lax.rem(chip + dc, chips) * 2 + core
@@ -464,69 +463,77 @@
     my_cols = pl.ds(pl.multiple_of(me * shard_len, LANES), shard_len)
     partner_cols = pl.ds(pl.multiple_of((chip * 2 + (1 - core)) * shard_len, LANES), shard_len)
 
-    def own_copies(n, cache, swap, last):
-        return [pltpu.make_async_copy(cache.at[me * rows + row], last.at[:, :, my_cols], own_sem.at[2 * n]),
-                pltpu.make_async_copy(swap.at[chip * rows + row], last.at[:, :, partner_cols], own_sem.at[2 * n + 1])]
-
-    def start(n, cache, swap, last):
+    def move(count):
+        def block(ref, index):
+            return ref.at[pl.ds(index * rows + rows - count, count)]
+
+        def remote(src, dst, device):
+            return pltpu.make_async_remote_copy(src_ref=src, dst_ref=dst, send_sem=k_send, recv_sem=k_recv, device_id={"sp": device}, device_id_type=MESH)
+
+        mine, partners = [k_last.at[pl.ds(2 - count, count), :, :, cols] for cols in (my_cols, partner_cols)]
         for own in (True, False):
             for dc in (2, 1, 3):
                 dst = same_core(dc)
-                src, cols = (cache.at[dst * rows + row], my_cols) if own else (swap.at[lax.rem(chip + dc, chips) * rows + row], partner_cols)
-                pltpu.make_async_remote_copy(src_ref=src, dst_ref=last.at[:, :, cols], send_sem=kv_send.at[n], recv_sem=kv_recv.at[n], device_id={"sp": dst}, device_id_type=MESH).start()
-        for copy in own_copies(n, cache, swap, last):
+                src = block(k_in, dst) if own else block(k_swap, lax.rem(chip + dc, chips))
+                remote(src, mine if own else partners, dst).start()
+        own_copies = [pltpu.make_async_copy(block(k_in, me), mine, own_sem.at[0]), pltpu.make_async_copy(block(k_swap, chip), partners, own_sem.at[1])]
+        for copy in own_copies:
             copy.start()
-
-    def finish(n, cache, swap, last):
-        for copy in own_copies(n, cache, swap, last):
+        for copy in own_copies:
             copy.wait()
-        ref = cache.at[pl.ds(0, 2 * (chips - 1))]
-        pltpu.make_async_remote_copy(src_ref=ref, dst_ref=ref, send_sem=kv_send.at[n], recv_sem=kv_recv.at[n], device_id={"sp": same_core(1)}, device_id_type=MESH).wait()
-
-    k_args, v_args = (0, k_in, k_swap, k_last), (1, v_in, v_swap, v_last)
+        total = k_in.at[pl.ds(0, 2 * (chips - 1) * count)]
+        remote(total, total, same_core(1)).wait()
 
     @pl.when(core == 0)
     def _():
-        start(*k_args)
-
-    start(*v_args)
+        move(2)
+
+    @pl.when(core == 1)
+    def _():
+        move(1)
+
+
+def put_kernel(hid, st, k_land, v_land, hid_dst, st_dst, k_dst, v_dst, sems):
+    rows, _, _, full_len = k_land.shape
+    tail = pl.ds(full_len - CACHE_EXTRA, CACHE_EXTRA)
+    core = lax.rem(lax.axis_index("sp"), 2)
+    pairs = [(v_land.at[row], v_dst.at[row]) for row in range(rows)] + [(k_land.at[row], k_dst.at[row]) for row in range(rows - 2)]
+    pairs += [(st, st_dst), (hid, hid_dst), (k_land.at[rows - 1, :, :, tail], k_dst.at[rows - 1, :, :, tail])]
+    copies = [pltpu.make_async_copy(src, dst, sems.at[n]) for n, (src, dst) in enumerate(pairs)]
+    for copy in copies:
+        copy.start()
+    row = rows - 2
+    whole = pltpu.make_async_copy(k_land.at[row], k_dst.at[row], sems.at[len(copies)])
+    part = pltpu.make_async_copy(k_land.at[row, :, :, tail], k_dst.at[row, :, :, tail], sems.at[len(copies)])
 
     @pl.when(core == 0)
     def _():
-        finish(*k_args)
-
-    finish(*v_args)
-
-
-def put_kernel(*refs):
-    count = (len(refs) - 1) // 2
-    sems = refs[-1]
-    copies = []
-    for n in (2, 3, 1, 0):
-        pieces = refs[n].shape[0] if n > 0 else 1
-        for i in range(pieces):
-            src, dst = (refs[n].at[i], refs[count + n].at[i]) if pieces > 1 else (refs[n], refs[count + n])
-            copies.append(pltpu.make_async_copy(src, dst, sems.at[len(copies)]))
-    for copy in copies:
-        copy.start()
+        part.start()
+        part.wait()
+
+    @pl.when(core == 1)
+    def _():
+        whole.start()
+        whole.wait()
+
     for copy in copies:
         copy.wait()
 
 
-def put_last_kernel(k_first, v_first, k_last, v_last, k_dst, v_dst, sems):
-    row = k_dst.shape[0] - 1
+def put_last_kernel(k_first, k_last, k_dst, sems):
+    rows = k_dst.shape[0]
     cols = pl.ds(0, k_last.shape[-1])
-    k_copy = pltpu.make_async_copy(k_last, k_dst.at[row, :, :, cols], sems.at[0])
-    v_copy = pltpu.make_async_copy(v_last, v_dst.at[row, :, :, cols], sems.at[1])
-    has_k = lax.rem(lax.axis_index("sp"), 2) == 0
-    v_copy.start()
-
-    @pl.when(has_k)
+    core = lax.rem(lax.axis_index("sp"), 2)
+    last = pltpu.make_async_copy(k_last.at[1], k_dst.at[rows - 1, :, :, cols], sems.at[0])
+    other = pltpu.make_async_copy(k_last.at[0], k_dst.at[rows - 2, :, :, cols], sems.at[1])
+    last.start()
+
+    @pl.when(core == 0)
     def _():
-        k_copy.start()
-        k_copy.wait()
-
-    v_copy.wait()
+        other.start()
+        other.wait()
+
+    last.wait()
 
 
 def solution(mesh):
@@ -624,27 +631,26 @@
             out_shape=[jax.ShapeDtypeStruct(shape, dtype) for shape, dtype in out_types],
             in_specs=[vmem] * 4,
             out_specs=[anym] * 4,
-            scratch_shapes=[dma((3 * rows + 1,))],
+            scratch_shapes=[dma((2 * rows + 2,))],
             compiler_params=pltpu.CompilerParams(vmem_limit_bytes=2 * 2 ** 20),
         )(*landed)
-        last_shape = (kv_dev, head_dim, prompt_len)
         last_rows = pl.pallas_call(
             functools.partial(last_kernel, dims),
-            out_shape=[pltpu.VMEM(last_shape, BF16)] * 2,
-            in_specs=[hbm] * 5,
-            out_specs=[vmem] * 2,
-            scratch_shapes=[dma((2,)), dma((2,)), dma((4,))],
+            out_shape=pltpu.VMEM((2, kv_dev, head_dim, prompt_len), BF16),
+            in_specs=[hbm] * 3,
+            out_specs=vmem,
+            scratch_shapes=[dma, dma, dma((2,))],
             compiler_params=pltpu.CompilerParams(collective_id=1, has_side_effects=True, vmem_limit_bytes=2 * 2 ** 20),
-        )(*in_hbm(k_cols, v_cols, k_swap, v_swap, hidden_out))
-        k_out, v_out = pl.pallas_call(
+        )(*in_hbm(k_cols, k_swap, hidden_out))
+        k_out = pl.pallas_call(
             put_last_kernel,
-            out_shape=[jax.ShapeDtypeStruct(shape, dtype) for shape, dtype in out_types[2:]],
-            in_specs=[hbm] * 2 + [vmem] * 2,
-            out_specs=[hbm] * 2,
+            out_shape=jax.ShapeDtypeStruct(land_shape, BF16),
+            in_specs=[hbm, vmem],
+            out_specs=hbm,
             scratch_shapes=[dma((2,))],
-            input_output_aliases={0: 0, 1: 1},
+            input_output_aliases={0: 0},
             compiler_params=pltpu.CompilerParams(vmem_limit_bytes=2 * 2 ** 20),
-        )(*in_hbm(k_out, v_out), *last_rows)
+        )(*in_hbm(k_out), last_rows)
         return hidden_out, state_new, jnp.transpose(k_out, (0, 1, 3, 2)), jnp.transpose(v_out, (0, 1, 3, 2))
 
     batch_spec = P(('dp', 'sp'), None)

time: 208 us -> 207 us (level)
  no operation moved by 1% of the time
where the time goes in v6:
time: 207 us; the launch traced here: 204 us
  Pallas kernels  203 us (98%)
    pallas_call x1, Pallas kernels, device_step(): pl.pallas_call(functools.partial(step_kernel, dims), out_shape=[pltpu.VME...  169 us
    pallas_call x1, Pallas kernels, device_step(): pl.pallas_call(functools.partial(last_kernel, dims), out_shape=pltpu.VMEM...  27.1 us
    pallas_call x1, Pallas kernels, device_step(): pl.pallas_call(put_kernel, out_shape=[jax.ShapeDtypeStruct(shape, dtype)...  5.73 us

profile of v6, /device:TPU:97, one launch (start us, length us, event | category | flops | bytes accessed | tf_op | source)
XLA Modules:
  0.0 204.1 jit_solution(4590763168510878035)
XLA Ops:
  0.6 169.3 %shard_map.165 = (bf16[4,2048]{1,0:T(4,128)(2,1)S(1)}, f32[4,8,64,64]{3,2,1,0:T(8,128)S(1)}, bf16[4,2,64,8208]{3,2,1,0:T(8,128)(2,1)S(1)}, bf16[4,2,64,8208]{3,2...) custom-call(bf16[4,2048]{1,0:T(4,128)(2,1)} %tok_in.1, f32[8]{0:T(128)} %slopes_in.1, ...), custom_call_target="tpu_custom_call" | custom-call | tf_op jit(solution)/shard_map/pallas_call | solution.py:616
  170.0 5.7 %shard_map.166 = (bf16[4,2048]{1,0:T(4,128)(2,1)}, f32[4,8,64,64]{3,2,1,0:T(8,128)}, bf16[4,2,64,8208]{3,2,1,0:T(8,128)(2,1)}, bf16[4,2,64,8208]{3,2,1,0:T(8,128)(2,1)}) custom-call(bf16[4,2048]{1,0:T(4,128)(2,1)S(1)} %get-tuple-element.13.hid, f32[4,8,64,64]{3,2,1,0:T(8,128)S(1)} %get-tuple-element.14.st, ...), custom_call_target="tpu_custom_call" | custom-call | tf_op jit(solution)/shard_map/pallas_call | solution.py:629
  175.7 27.1 %shard_map.167.k_last = bf16[2,2,64,8192]{3,2,1,0:T(8,128)(2,1)S(1)} custom-call(bf16[32,2,64,1024]{3,2,1,0:T(8,128)(2,1)} %bitcast.12, bf16[16,2,64,1024]{3,2,1,0:T(8,128)(2,1)} %get-tuple-element.20.k_swap, bf16[4,2048]{1,0:T(4,128)(2,1)} %get-tuple-element.9._), custom_call_target="tpu_custom_call" | custom-call | tf_op jit(solution)/shard_map/pallas_call | solution.py:637
  202.8 1.3 shard_map.168

commit v7 on v6

--- a/solution.py
+++ b/solution.py
@@ -471,11 +471,11 @@
             return pltpu.make_async_remote_copy(src_ref=src, dst_ref=dst, send_sem=k_send, recv_sem=k_recv, device_id={"sp": device}, device_id_type=MESH)
 
         mine, partners = [k_last.at[pl.ds(2 - count, count), :, :, cols] for cols in (my_cols, partner_cols)]
-        for own in (True, False):
-            for dc in (2, 1, 3):
+        for piece in range(count):
+            for dc, own in ((2, True), (1, True), (3, True), (2, False), (1, False), (3, False)):
                 dst = same_core(dc)
                 src = block(k_in, dst) if own else block(k_swap, lax.rem(chip + dc, chips))
-                remote(src, mine if own else partners, dst).start()
+                remote(src.at[piece], (mine if own else partners).at[piece], dst).start()
         own_copies = [pltpu.make_async_copy(block(k_in, me), mine, own_sem.at[0]), pltpu.make_async_copy(block(k_swap, chip), partners, own_sem.at[1])]
         for copy in own_copies:
             copy.start()

time: 207 us -> 207 us (level)
  no operation moved by 1% of the time
where the time goes in v7:
time: 207 us; the launch traced here: 205 us
  Pallas kernels  204 us (99%)
    pallas_call x1, Pallas kernels, device_step(): pl.pallas_call(functools.partial(step_kernel, dims), out_shape=[pltpu.VME...  169 us
    pallas_call x1, Pallas kernels, device_step(): pl.pallas_call(functools.partial(last_kernel, dims), out_shape=pltpu.VMEM...  27.7 us
    pallas_call x1, Pallas kernels, device_step(): pl.pallas_call(put_kernel, out_shape=[jax.ShapeDtypeStruct(shape, dtype)...  5.73 us

profile of v7, /device:TPU:97, one launch (start us, length us, event | category | flops | bytes accessed | tf_op | source)
XLA Modules:
  0.0 204.7 jit_solution(12654968678290508518)
XLA Ops:
  0.6 169.3 %shard_map.165 = (bf16[4,2048]{1,0:T(4,128)(2,1)S(1)}, f32[4,8,64,64]{3,2,1,0:T(8,128)S(1)}, bf16[4,2,64,8208]{3,2,1,0:T(8,128)(2,1)S(1)}, bf16[4,2,64,8208]{3,2...) custom-call(bf16[4,2048]{1,0:T(4,128)(2,1)} %tok_in.1, f32[8]{0:T(128)} %slopes_in.1, ...), custom_call_target="tpu_custom_call" | custom-call | tf_op jit(solution)/shard_map/pallas_call | solution.py:616
  170.0 5.7 %shard_map.166 = (bf16[4,2048]{1,0:T(4,128)(2,1)}, f32[4,8,64,64]{3,2,1,0:T(8,128)}, bf16[4,2,64,8208]{3,2,1,0:T(8,128)(2,1)}, bf16[4,2,64,8208]{3,2,1,0:T(8,128)(2,1)}) custom-call(bf16[4,2048]{1,0:T(4,128)(2,1)S(1)} %get-tuple-element.13.hid, f32[4,8,64,64]{3,2,1,0:T(8,128)S(1)} %get-tuple-element.14.st, ...), custom_call_target="tpu_custom_call" | custom-call | tf_op jit(solution)/shard_map/pallas_call | solution.py:629
  175.7 27.7 %shard_map.167.k_last = bf16[2,2,64,8192]{3,2,1,0:T(8,128)(2,1)S(1)} custom-call(bf16[32,2,64,1024]{3,2,1,0:T(8,128)(2,1)} %bitcast.12, bf16[16,2,64,1024]{3,2,1,0:T(8,128)(2,1)} %get-tuple-element.20.k_swap, bf16[4,2048]{1,0:T(4,128)(2,1)} %get-tuple-element.9._), custom_call_target="tpu_custom_call" | custom-call | tf_op jit(solution)/shard_map/pallas_call | solution.py:637
  203.4 1.3 shard_map.168
